TPU v7x, 32 devices: a 4x4x1 block of a 4x4x8 slice. The times are simulated.
32 devices in a mesh: rep: 2 (over z, core), dp: 16 (over x, y).
Axes of the slice: x: 4, y: 4, z: 1, core: 2. Of those that a mesh axis runs over, the one named last changes fastest.
The devices are a block of a 4x4x8 slice.
Arguments:
- x: bfloat16 [32, 4096, 512], P(('rep', 'dp')), parts along dimension 0
- dy: bfloat16 [32, 4096, 512], P(('rep', 'dp')), parts along dimension 0
- w_gate: bfloat16 [2, 512, 1408], P(None, 'dp')
- w_up: bfloat16 [2, 512, 1408], P(None, 'dp')
- w_down: bfloat16 [2, 1408, 512], P(None, 'dp')
Outputs:
- output 1: bfloat16 [32, 4096, 512], P(('rep', 'dp')), parts along dimension 0
- output 2: bfloat16 [4, 512, 1408], P('rep', 'dp'), parts along dimension 0
- output 3: bfloat16 [4, 512, 1408], P('rep', 'dp'), parts along dimension 0
- output 4: bfloat16 [4, 1408, 512], P('rep', 'dp'), parts along dimension 0
There are 2 independent parts. A program takes and returns all parts, laid end to end along the dimension named above; an argument that names none is the same for every part.
All inputs are finite; a program needn't handle non-finite values.
Results may differ from a plain program's by a relative error of at most 0.018.
Values are sent between devices in bfloat16 or wider.
A program may use at most 768 MiB of HBM per device.

v0:
```python
import jax
import jax.numpy as jnp
from jax import lax

NAMES = ("w_gate", "w_up", "w_down")


def matmul(a, w):
    return jnp.dot(a, w, preferred_element_type=jnp.float32).astype(jnp.bfloat16)


def normed(h):
    wide = h.astype(jnp.float32)
    scale = lax.rsqrt(jnp.mean(wide**2, -1, keepdims=True) + 1e-6)
    return (wide * scale).astype(jnp.bfloat16)


def layer(h, w):
    a = normed(h)
    gate = jnp.dot(a, w["w_gate"], preferred_element_type=jnp.float32)
    up = jnp.dot(a, w["w_up"], preferred_element_type=jnp.float32)
    return h + matmul((jax.nn.silu(gate) * up).astype(jnp.bfloat16), w["w_down"])


def stack(weights, h):
    for number in range(weights["w_gate"].shape[0]):
        h = layer(h, {name: w[number] for name, w in weights.items()})
    return h


def solution(mesh):
    groups = mesh.shape["rep"]

    def step(x, dy, *weights):
        shape = x.shape
        x, dy = (t.reshape(groups, -1, *t.shape[1:]) for t in (x, dy))

        def of_a_group(x, dy):
            _, back = jax.vjp(stack, dict(zip(NAMES, weights, strict=True)), x)
            by_weights, by_x = back(dy)
            return (by_x, *(by_weights[name] for name in NAMES))

        by_x, *by_weights = jax.vmap(of_a_group)(x, dy)
        return (by_x.reshape(shape), *(t.reshape(-1, *t.shape[2:]) for t in by_weights))

    return step
```

profile of v0, /device:TPU:96, one launch (start us, length us, event | category | flops | bytes accessed | tf_op | source)
XLA Modules:
  0.0 780.5 jit_solution(2341000040912320908)
XLA Ops:
  30.8 20.0 %all-gather.30.cloned.1.call-done = bf16[1,512,1408]{2,1,0:T(8,128)(2,1)} async-done(((bf16[1,32,1408]{2,1,0:T(8,128)(2,1)}), bf16[1,512,1408]{2,1,0:T(8,128)(2,1)}) %all-gather.30.cloned.1.call-update) | async-done | bytes 1441808 | tf_op jit(solution)/vmap(jvp())/squeeze | solution.py:27
  50.8 13.2 %fusion.102 = f32[4096,1408]{1,0:T(8,128)} fusion(bf16[1,4096,512]{2,1,0:T(8,128)(2,1)} %param.1, f32[4096]{0:T(1024)S(1)} %get-tuple-element.13, bf16[1,512,1408]{2,1,0:T(8,128)(2,1)} %all-gather.30.cloned.1.call-done), kind=kOutput, calls=%fused_computation.95 | convolution fusion | flops 5911871488 | bytes 28721152 | tf_op jit(solution)/vmap(jvp())/dot_general | solution.py:20
  64.0 27.0 %all-gather.32.cloned.1.call-done = bf16[1,512,1408]{2,1,0:T(8,128)(2,1)} async-done(((bf16[1,32,1408]{2,1,0:T(8,128)(2,1)}), bf16[1,512,1408]{2,1,0:T(8,128)(2,1)}) %all-gather.32.cloned.1.call-update) | async-done | bytes 1441808 | tf_op jit(solution)/vmap(jvp())/squeeze | solution.py:27
  91.0 16.1 %fusion.100 = f32[4096,1408]{1,0:T(8,128)} fusion(bf16[1,4096,512]{2,1,0:T(8,128)(2,1)} %param.1, f32[4096]{0:T(1024)S(1)} %get-tuple-element.13, bf16[1,512,1408]{2,1,0:T(8,128)(2,1)} %all-gather.32.cloned.1.call-done), kind=kOutput, calls=%fused_computation.94 | convolution fusion | flops 5911871488 | bytes 28721152 | tf_op jit(solution)/vmap(jvp())/dot_general | solution.py:21
  107.1 15.2 %fusion.26 = bf16[4096,1408]{1,0:T(8,128)(2,1)} fusion(f32[4096,1408]{1,0:T(8,128)} %fusion.100, f32[4096,1408]{1,0:T(8,128)S(1)} %copy-done), kind=kLoop, calls=%fused_computation.45 | loop fusion | flops 34603008 | bytes 57671680
  122.2 8.4 %all-gather.34.cloned.1.call-done = bf16[1,1408,512]{2,1,0:T(8,128)(2,1)} async-done(((bf16[1,88,512]{2,1,0:T(8,128)(2,1)}), bf16[1,1408,512]{2,1,0:T(8,128)(2,1)}) %all-gather.34.cloned.1.call-update) | async-done | bytes 1441808 | tf_op jit(solution)/vmap(jvp())/squeeze | solution.py:27
  130.6 12.5 %fusion.38 = (f32[4096]{0:T(1024)S(1)}, bf16[1,1,4096,512]{2,3,1,0:T(8,128)(2,1)}) fusion(bf16[4096,1408]{1,0:T(8,128)(2,1)} %fusion.26, bf16[1,1408,512]{2,1,0:T(8,128)(2,1)} %all-gather.34.cloned.1.call-done, bf16[1,4096,512]{1,2,0:T(8,128)(2,1)} %copy.1), kind=kOutput, calls=%fused_computation.60 | convolution fusion | flops 5916061696 | bytes 21381120 | tf_op jit(solution)/vmap(jvp())/dot_general | solution.py:9
  143.1 27.5 %all-gather.36.cloned.1.call-done = bf16[1,512,1408]{2,1,0:T(8,128)(2,1)} async-done(((bf16[1,32,1408]{2,1,0:T(8,128)(2,1)}), bf16[1,512,1408]{2,1,0:T(8,128)(2,1)}) %all-gather.36.cloned.1.call-update) | async-done | bytes 1441808 | tf_op jit(solution)/vmap(jvp())/squeeze | solution.py:27
  170.6 13.3 %fusion.98 = f32[4096,1408]{1,0:T(8,128)} fusion(bf16[1,1,4096,512]{2,3,1,0:T(8,128)(2,1)} %get-tuple-element.15, f32[4096]{0:T(1024)S(1)} %bitcast.283, bf16[1,512,1408]{2,1,0:T(8,128)(2,1)} %all-gather.36.cloned.1.call-done), kind=kOutput, calls=%fused_computation.93 | convolution fusion | flops 5911871488 | bytes 28721152 | tf_op jit(solution)/vmap(jvp())/dot_general | solution.py:20
  183.9 26.7 %all-gather.40.cloned.1.call-done = bf16[1,512,1408]{2,1,0:T(8,128)(2,1)} async-done(((bf16[1,32,1408]{2,1,0:T(8,128)(2,1)}), bf16[1,512,1408]{2,1,0:T(8,128)(2,1)}) %all-gather.40.cloned.1.call-update) | async-done | bytes 1441808 | tf_op jit(solution)/vmap(jvp())/squeeze | solution.py:27
  210.6 13.1 %fusion.96 = f32[4096,1408]{1,0:T(8,128)} fusion(bf16[1,1,4096,512]{2,3,1,0:T(8,128)(2,1)} %get-tuple-element.15, f32[4096]{0:T(1024)S(1)} %bitcast.284, bf16[1,512,1408]{2,1,0:T(8,128)(2,1)} %all-gather.40.cloned.1.call-done), kind=kOutput, calls=%fused_computation.92 | convolution fusion | flops 5911871488 | bytes 28721152 | tf_op jit(solution)/vmap(jvp())/dot_general | solution.py:21
  223.8 26.3 %all-gather.38.cloned.1.call-done = bf16[1,1408,512]{2,1,0:T(8,128)(2,1)} async-done(((bf16[1,88,512]{2,1,0:T(8,128)(2,1)}), bf16[1,1408,512]{2,1,0:T(8,128)(2,1)}) %all-gather.38.cloned.1.call-update) | async-done | bytes 1441808 | tf_op jit(solution)/vmap(jvp())/squeeze | solution.py:27
  250.1 12.0 %fusion.24 = bf16[1,1,4096,1408]{3,2,1,0:T(8,128)(2,1)} fusion(bf16[1,4096,512]{2,1,0:T(8,128)(2,1)} %param, bf16[1,1408,512]{2,1,0:T(8,128)(2,1)} %all-gather.38.cloned.1.call-done), kind=kOutput, calls=%fused_computation.40 | convolution fusion | flops 5911347200 | bytes 17170432 | tf_op jit(solution)/vmap(transpose(jvp()))/dot_general | solution.py:9
  263.5 19.0 %fusion.4 = bf16[4096,1408]{1,0:T(8,128)(2,1)} fusion(f32[4096,1408]{1,0:T(8,128)S(1)} %copy-done.1, f32[4096,1408]{1,0:T(8,128)} %fusion.96, bf16[1,1,4096,1408]{3,2,1,0:T(8,128)(2,1)} %fusion.24), kind=kLoop, calls=%fused_computation.10 | loop fusion | flops 69206016 | bytes 69206016
  282.5 13.2 %convolution_convert_fusion.4 = bf16[4096,512]{0,1:T(8,128)(2,1)} fusion(bf16[4096,1408]{1,0:T(8,128)(2,1)} %fusion.4, bf16[1,512,1408]{2,1,0:T(8,128)(2,1)S(1)} %copy-done.7), kind=kOutput, calls=%fused_computation.67 | convolution fusion | flops 5905580032 | bytes 17170432 | tf_op jit(solution)/vmap(transpose(jvp()))/dot_general | solution.py:20
  295.7 19.5 %fusion.40 = (f32[4096]{0:T(1024)S(1)}, bf16[1,1,4096,512]{2,3,1,0:T(8,128)(2,1)}) fusion(bf16[1,1,4096,512]{2,3,1,0:T(8,128)(2,1)} %get-tuple-element.15, bf16[4096,512]{0,1:T(8,128)(2,1)} %convolution_convert_fusion.4, bf16[1,512,1408]{2,1,0:T(8,128)(2,1)S(1)} %copy-done.8, bf16[1,1,4096,1408]{3,2,1,0:T(8,128)(2,1)} %fusion.24, f32[4096,1408]{1,0:T(8,128)} %fusion.98), kind=kOutput, calls=%fused_computation.62 | convolution fusion | flops 5952761856 | bytes 48644096 | tf_op jit(solution)/vmap(transpose(jvp()))/dot_general | solution.py:21
  323.4 10.7 %fusion.91 = f32[1,1408,512]{2,1,0:T(8,128)} fusion(bf16[4096,1408]{1,0:T(8,128)(2,1)} %fusion.26, bf16[1,1,4096,512]{2,3,1,0:T(8,128)(2,1)S(1)} %fusion.65), kind=kOutput, calls=%fused_computation.91 | convolution fusion | flops 5905580032 | bytes 18612224 | tf_op jit(solution)/vmap(transpose(jvp()))/dot_general | solution.py:9
  334.2 20.9 %fusion.78 = f32[1,1408,512]{2,1,0:T(8,128)} fusion(bf16[1,4096,512]{2,1,0:T(8,128)(2,1)} %param, f32[4096,1408]{1,0:T(8,128)} %fusion.96, f32[4096,1408]{1,0:T(8,128)} %fusion.98), kind=kOutput, calls=%fused_computation.87 | convolution fusion | flops 5940183040 | bytes 53215232 | tf_op jit(solution)/vmap(transpose(jvp()))/dot_general | solution.py:9
  355.1 17.5 %fusion.83 = f32[1,512,1408]{2,1,0:T(8,128)} fusion(bf16[1,1,4096,1408]{3,2,1,0:T(8,128)(2,1)} %fusion.24, f32[4096,1408]{1,0:T(8,128)} %fusion.98, bf16[1,1,4096,512]{2,3,1,0:T(8,128)(2,1)} %get-tuple-element.15, f32[4096]{0:T(1024)S(1)} %bitcast.286), kind=kOutput, calls=%fused_computation.88 | convolution fusion | flops 5946474496 | bytes 41697280 | tf_op jit(solution)/vmap(transpose(jvp()))/dot_general | solution.py:21
  372.8 9.3 %fusion.25 = bf16[1,1,4096,1408]{3,2,1,0:T(8,128)(2,1)S(1)} fusion(bf16[1,1,4096,512]{2,3,1,0:T(8,128)(2,1)} %copy-done.2, bf16[1,1408,512]{2,1,0:T(8,128)(2,1)S(1)} %copy-done.6), kind=kOutput, calls=%fused_computation.41 | convolution fusion | flops 5911347200 | bytes 17170432 | tf_op jit(solution)/vmap(transpose(jvp()))/dot_general | solution.py:9
  386.2 21.1 %fusion.7 = bf16[4096,1408]{1,0:T(8,128)(2,1)} fusion(f32[4096,1408]{1,0:T(8,128)} %fusion.102, f32[4096,1408]{1,0:T(8,128)} %fusion.100, bf16[1,1,4096,1408]{3,2,1,0:T(8,128)(2,1)S(1)} %fusion.25), kind=kLoop, calls=%fused_computation.13 | loop fusion | flops 69206016 | bytes 69206016
  407.5 12.8 %convolution_convert_fusion.3 = bf16[4096,512]{0,1:T(8,128)(2,1)} fusion(bf16[4096,1408]{1,0:T(8,128)(2,1)} %fusion.7, bf16[1,512,1408]{2,1,0:T(8,128)(2,1)S(1)} %copy-done.5), kind=kOutput, calls=%fused_computation.66 | convolution fusion | flops 5905580032 | bytes 17170432 | tf_op jit(solution)/vmap(transpose(jvp()))/dot_general | solution.py:20
  420.3 20.5 %fusion.36 = (f32[4096]{0:T(1024)S(1)}, bf16[1,1,4096,512]{2,3,1,0:T(8,128)(2,1)}) fusion(bf16[1,4096,512]{1,2,0:T(8,128)(2,1)} %copy.1, bf16[4096,512]{0,1:T(8,128)(2,1)} %convolution_convert_fusion.3, bf16[1,512,1408]{2,1,0:T(8,128)(2,1)} %all-gather.32.cloned.1.call-done, bf16[1,1,4096,1408]{3,2,1,0:T(8,128)(2,1)} %copy-done.3, f32[4096,1408]{1,0:T(8,128)} %fusion.102), kind=kOutput, calls=%fused_computation.58 | convolution fusion | flops 5952761856 | bytes 48644096 | tf_op jit(solution)/vmap(transpose(jvp()))/dot_general | solution.py:21
  440.9 17.4 %fusion.86 = f32[1,512,1408]{2,1,0:T(8,128)} fusion(bf16[1,1,4096,1408]{3,2,1,0:T(8,128)(2,1)} %copy-done.3, f32[4096,1408]{1,0:T(8,128)} %fusion.102, bf16[1,4096,512]{1,2,0:T(8,128)(2,1)} %copy.1, f32[4096]{0:T(1024)S(1)} %bitcast.288), kind=kOutput, calls=%fused_computation.89 | convolution fusion | flops 5946474496 | bytes 41697280 | tf_op jit(solution)/vmap(transpose(jvp()))/dot_general | solution.py:21
  458.4 12.2 %convolution_bitcast_fusion = f32[1,512,1408]{2,1,0:T(8,128)} fusion(bf16[4096,1408]{1,0:T(8,128)(2,1)} %fusion.4, bf16[1,1,4096,512]{2,3,1,0:T(8,128)(2,1)} %get-tuple-element.15, f32[4096]{0:T(1024)S(1)} %bitcast.287), kind=kOutput, calls=%fused_computation.90 | convolution fusion | flops 5911871488 | bytes 18628608 | tf_op jit(solution)/vmap(transpose(jvp()))/dot_general | solution.py:20
  470.8 12.0 %fusion.75 = f32[1,512,1408]{2,1,0:T(8,128)} fusion(bf16[4096,1408]{1,0:T(8,128)(2,1)} %fusion.7, bf16[1,4096,512]{1,2,0:T(8,128)(2,1)} %copy.1, f32[4096]{0:T(1024)S(1)} %bitcast.289), kind=kOutput, calls=%fused_computation.86 | convolution fusion | flops 5911871488 | bytes 18628608 | tf_op jit(solution)/vmap(transpose(jvp()))/dot_general | solution.py:20
  482.8 7.6 fusion.64
  490.4 6.4 copy.2
  499.4 52.1 %reduce-scatter.27.cloned.1.call-done = f32[1,32,1408]{2,1,0:T(8,128)} async-done(((f32[1,512,1408]{2,1,0:T(8,128)}), f32[1,32,1408]{2,1,0:T(8,128)}) %reduce-scatter.27.cloned.1.call-update) | async-done | bytes 180240
  552.5 72.3 %reduce-scatter.29.cloned.1.call-done = f32[1,32,1408]{2,1,0:T(8,128)} async-done(((f32[1,512,1408]{2,1,0:T(8,128)}), f32[1,32,1408]{2,1,0:T(8,128)}) %reduce-scatter.29.cloned.1.call-update) | async-done | bytes 180240
  626.4 71.9 %reduce-scatter.23.cloned.1.call-done = f32[1,32,1408]{2,1,0:T(8,128)} async-done(((f32[1,512,1408]{2,1,0:T(8,128)}), f32[1,32,1408]{2,1,0:T(8,128)}) %reduce-scatter.23.cloned.1.call-update) | async-done | bytes 180240
  699.3 72.3 %reduce-scatter.25.cloned.1.call-done = f32[1,32,1408]{2,1,0:T(8,128)} async-done(((f32[1,512,1408]{2,1,0:T(8,128)}), f32[1,32,1408]{2,1,0:T(8,128)}) %reduce-scatter.25.cloned.1.call-update) | async-done | bytes 180240
  (65 shorter events, 45.6 us)
Async XLA Ops:
  7.2 43.6 %all-gather.30.cloned.1.call-start = ((), (), s32[]{:S(2)}) async-start(), calls=%async_computation.6 | async-start | bytes 1531904 | tf_op jit(solution)/vmap(jvp())/squeeze | solution.py:27
  8.9 82.1 %all-gather.32.cloned.1.call-start = ((), (), s32[]{:S(2)}) async-start(), calls=%async_computation.7 | async-start | bytes 1531904 | tf_op jit(solution)/vmap(jvp())/squeeze | solution.py:27
  10.7 119.9 %all-gather.34.cloned.1.call-start = ((), (), s32[]{:S(2)}) async-start(), calls=%async_computation.8 | async-start | bytes 1531904 | tf_op jit(solution)/vmap(jvp())/squeeze | solution.py:27
  12.4 158.2 %all-gather.36.cloned.1.call-start = ((), (), s32[]{:S(2)}) async-start(), calls=%async_computation.9 | async-start | bytes 1531904 | tf_op jit(solution)/vmap(jvp())/squeeze | solution.py:27
  13.1 197.6 %all-gather.40.cloned.1.call-start = ((), (), s32[]{:S(2)}) async-start(), calls=%async_computation.11 | async-start | bytes 1531904 | tf_op jit(solution)/vmap(jvp())/squeeze | solution.py:27
  13.7 236.4 %all-gather.38.cloned.1.call-start = ((), (), s32[]{:S(2)}) async-start(), calls=%async_computation.10 | async-start | bytes 1531904 | tf_op jit(solution)/vmap(jvp())/squeeze | solution.py:27
  14.3 482.5 %reduce-scatter.33.cloned.1.call-start = ((), (), s32[]{:S(2)}) async-start(), calls=%async_computation.17 | async-start | bytes 3063808
  91.0 16.1 %copy-start = (f32[4096,1408]{1,0:T(8,128)S(1)}, f32[4096,1408]{1,0:T(8,128)}, u32[]{:S(2)}) copy-start(f32[4096,1408]{1,0:T(8,128)} %fusion.102) | copy-start | bytes 69206016
  250.1 13.4 %copy-start.1 = (f32[4096,1408]{1,0:T(8,128)S(1)}, f32[4096,1408]{1,0:T(8,128)}, u32[]{:S(2)}) copy-start(f32[4096,1408]{1,0:T(8,128)} %fusion.98) | copy-start | bytes 69206016
  263.5 19.0 %copy-start.7 = (bf16[1,512,1408]{2,1,0:T(8,128)(2,1)S(1)}, bf16[1,512,1408]{2,1,0:T(8,128)(2,1)}, u32[]{:S(2)}) copy-start(bf16[1,512,1408]{2,1,0:T(8,128)(2,1)} %all-gather.36.cloned.1.call-done) | copy-start | bytes 4325380
  282.5 13.2 %copy-start.8 = (bf16[1,512,1408]{2,1,0:T(8,128)(2,1)S(1)}, bf16[1,512,1408]{2,1,0:T(8,128)(2,1)}, u32[]{:S(2)}) copy-start(bf16[1,512,1408]{2,1,0:T(8,128)(2,1)} %all-gather.40.cloned.1.call-done) | copy-start | bytes 4325380
  321.4 2.0 copy-start.2
  334.1 163.7 %reduce-scatter.31.cloned.1.call-start = ((), (), s32[]{:S(2)}) async-start(), calls=%async_computation.16 | async-start | bytes 3063808
  355.1 17.6 %copy-start.6 = (bf16[1,1408,512]{2,1,0:T(8,128)(2,1)S(1)}, bf16[1,1408,512]{2,1,0:T(8,128)(2,1)}, u32[]{:S(2)}) copy-start(bf16[1,1408,512]{2,1,0:T(8,128)(2,1)} %all-gather.34.cloned.1.call-done) | copy-start | bytes 4325380
  372.7 178.8 %reduce-scatter.27.cloned.1.call-start = ((), (), s32[]{:S(2)}) async-start(), calls=%async_computation.14 | async-start | bytes 3063808
  382.1 4.2 copy-start.3
  386.2 21.2 %copy-start.5 = (bf16[1,512,1408]{2,1,0:T(8,128)(2,1)S(1)}, bf16[1,512,1408]{2,1,0:T(8,128)(2,1)}, u32[]{:S(2)}) copy-start(bf16[1,512,1408]{2,1,0:T(8,128)(2,1)} %all-gather.30.cloned.1.call-done) | copy-start | bytes 4325380
  407.4 217.4 %reduce-scatter.29.cloned.1.call-start = ((), (), s32[]{:S(2)}) async-start(), calls=%async_computation.15 | async-start | bytes 3063808
  420.3 20.5 %copy-start.4 = (f32[4096]{0:T(1024)S(1)}, f32[4096]{0:T(1024)}, u32[]{:S(2)}) copy-start(f32[4096]{0:T(1024)} %get-tuple-element.12) | copy-start | bytes 49156
  458.3 240.0 %reduce-scatter.23.cloned.1.call-start = ((), (), s32[]{:S(2)}) async-start(), calls=%async_computation.12 | async-start | bytes 3063808
  470.7 300.9 %reduce-scatter.25.cloned.1.call-start = ((), (), s32[]{:S(2)}) async-start(), calls=%async_computation.13 | async-start | bytes 3063808
Sparse Core Ops, SparseCore 0:
  10.0 40.7 all-gather.29
  53.4 37.5 all-gather.31
  93.0 37.5 all-gather.33
  133.0 37.5 all-gather.35
  173.0 37.5 all-gather.39
  212.5 37.5 all-gather.37
  334.2 70.2 reduce-scatter.32
  407.7 70.3 reduce-scatter.30
  481.2 70.2 reduce-scatter.26
  554.5 70.2 reduce-scatter.28
  628.0 70.3 reduce-scatter.22
  701.4 70.1 reduce-scatter.24
where the time goes:
time: 790 us; the launch traced here: 781 us
  waiting for transfers between devices  407 us (52%)
  matrix products  246 us (31%)
  other arithmetic  80.4 us (10%)
  local copies, waits for them, and re-layouts  31.5 us (4%)
  between operations  14.8 us (2%)
    unnamed x18, waiting for transfers between devices  271 us
    squeeze x6, waiting for transfers between devices, stack(): h = layer(h, {name: w[number] for name, w in weights.items()})  136 us
    dot_general x6, matrix products, layer(): up = jnp.dot(a, w['w_up'], preferred_element_type=jnp.float32)  104 us
    dot_general x6, matrix products, layer(): gate = jnp.dot(a, w['w_gate'], preferred_element_type=jnp.float32)  76.7 us
    dot_general x5, matrix products, matmul(): jnp.dot(a, w, preferred_element_type=jnp.float32).astype(jnp.bfloat16)  65.4 us
    unnamed x3, other arithmetic  55.3 us
    unnamed x21, local copies, waits for them, and re-layouts  26.6 us
  transfers between devices with their start and end apart: 12, of which 10 were waited for; matrix products, arithmetic and copies ran while one was open for 34% of the time, Pallas kernels for 0%

commit v1 on v0

v1 whole, which is shorter than its diff:
```python
import functools
import math

import jax
import jax.numpy as jnp
from jax import lax
from jax.experimental import pallas as pl
from jax.experimental.pallas import tpu as pltpu
from jax.sharding import PartitionSpec as P

bf16, f32 = jnp.bfloat16, jnp.float32
MESH = pl.DeviceIdType.MESH
TILE = 512
CHUNK = 256
STEPS = 4
DIMS = ((1, 0), (0, 1), (3, 0), (0, 3))


def dot(a, b):
    return jnp.dot(a, b, preferred_element_type=f32)


def dot_t(a, b):
    return lax.dot_general(a, b, (((0,), (0,)), ((), ())), preferred_element_type=f32)


def flip(c, bits):
    return (c, c + 1 - 2 * lax.rem(c, 2), lax.rem(c + 2, 4), 3 - c)[bits]


def mask_of(part, slot):
    x = y = 0
    for bit in range(STEPS):
        if slot >> bit & 1:
            dx, dy = DIMS[(part + STEPS - 1 - bit) % 4]
            x, y = x ^ dx, y ^ dy
    return x, y


def kernel(sizes, x_hbm, dy_hbm, wg_ref, wu_ref, wd_ref, dx_hbm, og_ref, ou_ref, od_ref, *scratch):
    (x_s, h_s, dy_s, wgu, wd0, wgut, wdt, acc_gu, acc_d, p_s, dgu_s, *rest) = scratch
    slots = (rest[:8], rest[8:16])
    send_sem, recv_sem, credit, copy_sem, out_sem = rest[16:]
    tokens, width, hidden, deep, share_gu, share_d = sizes
    me = lax.axis_index("dp")
    mx, my = lax.div(me, 4), lax.rem(me, 4)

    def device(mask):
        return flip(mx, mask[0]) * 4 + flip(my, mask[1])

    lanes = 2 * hidden // 128
    cuts = [128 * (lanes * q // 4) for q in range(5)]
    cols_gu = list(zip(cuts, cuts[1:]))
    cols_d = [(width * q // 4, width * (q + 1) // 4) for q in range(4)]
    cols = cols_gu + cols_d

    copies = [pltpu.make_async_copy(x_hbm, x_s, copy_sem.at[0]), pltpu.make_async_copy(dy_hbm, dy_s, copy_sem.at[1])]
    for copy in copies:
        copy.start()

    barrier = pltpu.get_barrier_semaphore()
    for dim in DIMS:
        pl.semaphore_signal(barrier, inc=1, device_id={"dp": device(dim)}, device_id_type=MESH)

    def gate_up(ref_g, ref_u, layer, lo, hi):
        pieces = []
        if lo < hidden:
            pieces.append(ref_g[layer, :, lo:min(hi, hidden)])
        if hi > hidden:
            pieces.append(ref_u[layer, :, max(lo, hidden) - hidden:hi - hidden])
        return pieces

    def own_blocks(layer):
        for q, (lo, hi) in enumerate(cols_gu):
            at = 0
            for piece in gate_up(wg_ref, wu_ref, layer, lo, hi):
                slots[layer][q][0, :, at:at + piece.shape[1]] = piece
                at += piece.shape[1]
        for q, (lo, hi) in enumerate(cols_d):
            slots[layer][4 + q][0] = wd_ref[layer, :, lo:hi]

    def gather_copy(layer, step, a):
        q, n = a % 4, 2**step
        return pltpu.make_async_remote_copy(
            src_ref=slots[layer][a].at[pl.ds(0, n)], dst_ref=slots[layer][a].at[pl.ds(n, n)],
            send_sem=send_sem.at[layer, a, step], recv_sem=recv_sem.at[layer, a, step],
            device_id={"dp": device(DIMS[(q + STEPS - 1 - step) % 4])}, device_id_type=MESH)

    def gather_start(layer, step):
        for a in range(8):
            gather_copy(layer, step, a).start()

    def gather_wait(layer, step):
        for a in range(8):
            gather_copy(layer, step, a).wait()

    def install(layer):
        for r in range(16):
            for a, (lo, hi) in enumerate(cols):
                owner = device(mask_of(a % 4, r))
                if a < 4:
                    wgu[layer, pl.ds(pl.multiple_of(owner * share_gu, share_gu), share_gu), lo:hi] = slots[layer][a][r]
                else:
                    acc_d[layer, pl.ds(pl.multiple_of(owner * share_d, 8), share_d), lo:hi] = slots[layer][a][r].astype(f32)

    def scatter_copy(layer, step, a):
        q, n = a % 4, 2 ** (STEPS - 1 - step)
        return pltpu.make_async_remote_copy(
            src_ref=slots[1][a].at[pl.ds(n, n)], dst_ref=slots[0][a].at[pl.ds(n, n)],
            send_sem=send_sem.at[2 + layer, a, step], recv_sem=recv_sem.at[2 + layer, a, step],
            device_id={"dp": device(DIMS[(q + step) % 4])}, device_id_type=MESH)

    def scatter_start(layer, step):
        for a in range(8):
            if layer == 0:
                pl.semaphore_wait(credit.at[a, step], 1)
            scatter_copy(layer, step, a).start()

    def scatter_fill(layer):
        for r in range(8, 16):
            for a, (lo, hi) in enumerate(cols):
                acc, share = (acc_gu, share_gu) if a < 4 else (acc_d, share_d)
                owner = device(mask_of(a % 4, r))
                slots[1][a][r] = acc[layer, pl.ds(pl.multiple_of(owner * share, 8), share), lo:hi].astype(bf16)

    def scatter_add(layer, step):
        n = 2 ** (STEPS - 1 - step)
        for a, (lo, hi) in enumerate(cols):
            scatter_copy(layer, step, a).wait()
            acc, share = (acc_gu, share_gu) if a < 4 else (acc_d, share_d)
            for r in range(n):
                rows = pl.ds(pl.multiple_of(device(mask_of(a % 4, r)) * share, 8), share)
                total = acc[layer, rows, lo:hi] + slots[0][a][n + r].astype(f32)
                if n == 1:
                    total = total.astype(bf16)
                    if a >= 4:
                        od_ref[layer, :, lo:hi] = total
                    else:
                        if lo < hidden:
                            og_ref[layer, :, lo:min(hi, hidden)] = total[:, :min(hi, hidden) - lo]
                        if hi > hidden:
                            ou_ref[layer, :, max(lo, hidden) - hidden:hi - hidden] = total[:, max(lo, hidden) - lo:]
                elif r >= n // 2:
                    slots[1][a][r] = total.astype(bf16)
                else:
                    acc[layer, rows, lo:hi] = total
            if layer == 1:
                pl.semaphore_signal(credit.at[a, step], inc=1, device_id={"dp": device(DIMS[(a + step) % 4])}, device_id_type=MESH)

    chunks = [(lo, min(lo + CHUNK, hidden)) for lo in range(0, hidden, CHUNK)]

    def normed(ref, rows):
        wide = ref[rows, :].astype(f32)
        scale = lax.rsqrt(jnp.mean(wide * wide, -1, keepdims=True) + 1e-6)
        return wide, scale, (wide * scale).astype(bf16)

    def at_tile(i):
        return pl.ds(pl.multiple_of(i * TILE, TILE), TILE)

    def transposes(layer, down):
        for lo in range(0, 2 * hidden, CHUNK):
            wgut[lo:lo + CHUNK, :] = wgu[layer, :, lo:lo + CHUNK].T
        for lo, hi in chunks:
            wdt[:, lo:hi] = down[lo:hi, :].T.astype(bf16)

    def backward(layer, i, h_ref, dy_ref, out_ref):
        rows = at_tile(i)
        wide, scale, a = normed(h_ref, rows)
        dy = dy_ref[rows, :]
        for lo, hi in chunks:
            g, u = dot(a, wgu[layer, :, lo:hi]), dot(a, wgu[layer, :, hidden + lo:hidden + hi])
            dq = dot(dy, wdt[:, lo:hi]).astype(bf16).astype(f32)
            sig = 0.5 * jnp.tanh(0.5 * g) + 0.5
            s = g * sig
            p_s[:, lo:hi] = (s * u).astype(bf16)
            dgu_s[:, hidden + lo:hidden + hi] = (dq * s).astype(bf16)
            dgu_s[:, lo:hi] = (dq * u * (sig + s * (1 - sig))).astype(bf16)
        acc_d[layer] += dot_t(p_s[...], dy)
        acc_gu[layer] += dot_t(a, dgu_s[...])
        da = dot(dgu_s[...], wgut[...]).astype(bf16).astype(f32)
        mean = jnp.mean(da * wide, -1, keepdims=True)
        out_ref[rows, :] = dy + (da * scale - wide * (mean * scale * scale * scale)).astype(bf16)

    own_blocks(0)
    own_blocks(1)
    pl.semaphore_wait(barrier, 4)
    for step in range(STEPS):
        gather_start(0, step)
        gather_wait(0, step)
    gather_start(1, 0)
    install(0)
    wd0[...] = acc_d[0].astype(bf16)
    for copy in copies:
        copy.wait()

    def forward(i, _):
        for step, when in enumerate((2, 4, 7)):
            @pl.when(i == when)
            def _():
                gather_wait(1, step)
                gather_start(1, step + 1)
        rows = at_tile(i)
        _, _, a = normed(x_s, rows)
        for lo, hi in chunks:
            g, u = dot(a, wgu[0, :, lo:hi]), dot(a, wgu[0, :, hidden + lo:hidden + hi])
            p_s[:, lo:hi] = (g * (0.5 * jnp.tanh(0.5 * g) + 0.5) * u).astype(bf16)
        h_s[rows, :] = x_s[rows, :] + dot(p_s[...], wd0[...]).astype(bf16)
        return 0

    tiles = tokens // TILE
    lax.fori_loop(0, tiles, forward, 0)
    gather_wait(1, STEPS - 1)
    install(1)
    transposes(1, acc_d.at[1])
    acc_gu[...] = jnp.zeros_like(acc_gu)
    acc_d[...] = jnp.zeros_like(acc_d)

    def last(i, _):
        backward(1, i, h_s, dy_s, h_s)
        return 0

    lax.fori_loop(0, tiles, last, 0)
    scatter_fill(1)
    scatter_start(1, 0)
    transposes(0, wd0)

    def out_copy(i):
        return pltpu.make_async_copy(x_s.at[at_tile(i)], dx_hbm.at[at_tile(i)], out_sem.at[i])

    def first(i, _):
        for step, when in enumerate((2, 4, 5, 6)):
            @pl.when(i == when)
            def _():
                scatter_add(1, step)
                if step < STEPS - 1:
                    scatter_start(1, step + 1)
        backward(0, i, x_s, h_s, x_s)
        out_copy(i).start()
        return 0

    lax.fori_loop(0, tiles, first, 0)
    scatter_fill(0)
    for step in range(STEPS):
        scatter_start(0, step)
        scatter_add(0, step)
    for i in range(tiles):
        out_copy(i).wait()


def solution(mesh):
    group = mesh.shape["dp"]
    side = math.isqrt(group)
    assert side * side == group == 2**STEPS

    def local(x, dy, w_gate, w_up, w_down):
        _, tokens, width = x.shape
        layers, share_gu, hidden = w_gate.shape
        share_d = w_down.shape[1]
        lanes = 2 * hidden // 128
        cuts = [128 * (lanes * q // 4) for q in range(5)]
        parts = [pltpu.VMEM((group, share_gu, hi - lo), bf16) for lo, hi in zip(cuts, cuts[1:])]
        parts += [pltpu.VMEM((group, share_d, width // 4), bf16)] * 4
        any_, vmem = pl.BlockSpec(memory_space=pl.ANY), pl.BlockSpec(memory_space=pltpu.VMEM)
        out = pl.pallas_call(
            functools.partial(kernel, (tokens, width, hidden, layers, share_gu, share_d)),
            out_shape=[jax.ShapeDtypeStruct(s, bf16) for s in ((tokens, width), w_gate.shape, w_up.shape, w_down.shape)],
            in_specs=[any_, any_, vmem, vmem, vmem],
            out_specs=[any_, vmem, vmem, vmem],
            scratch_shapes=[pltpu.VMEM((tokens, width), bf16)] * 3 + [
                pltpu.VMEM((layers, width, 2 * hidden), bf16),
                pltpu.VMEM((hidden, width), bf16),
                pltpu.VMEM((2 * hidden, width), bf16),
                pltpu.VMEM((width, hidden), bf16),
                pltpu.VMEM((layers, width, 2 * hidden), f32),
                pltpu.VMEM((layers, hidden, width), f32),
                pltpu.VMEM((TILE, hidden), bf16),
                pltpu.VMEM((TILE, 2 * hidden), bf16),
            ] + parts * 2 + [
                pltpu.SemaphoreType.DMA((4, 8, STEPS)),
                pltpu.SemaphoreType.DMA((4, 8, STEPS)),
                pltpu.SemaphoreType.REGULAR((8, STEPS)),
                pltpu.SemaphoreType.DMA((2,)),
                pltpu.SemaphoreType.DMA((tokens // TILE,)),
            ],
            compiler_params=pltpu.CompilerParams(collective_id=0, has_side_effects=True, vmem_limit_bytes=67043328),
            name="stack",
        )(x[0], dy[0], w_gate, w_up, w_down)
        return (out[0][None], *out[1:])

    tokens_spec = P(("rep", "dp"), None, None)
    weight_spec, grad_spec = P(None, "dp", None), P("rep", "dp", None)
    return jax.shard_map(local, mesh=mesh, in_specs=(tokens_spec, tokens_spec) + (weight_spec,) * 3,
                         out_specs=(tokens_spec,) + (grad_spec,) * 3, check_vma=False)
```

time: 790 us -> 220 us (0.28); the launches traced: 781 us -> 219 us
  waiting for transfers between devices: 407 us -> 0 us
  matrix products: 246 us -> 0 us
  Pallas kernels: 0 us -> 211 us
  other arithmetic: 80.4 us -> 0 us
  local copies, waits for them, and re-layouts: 31.5 us -> 6.55 us
  between operations: 14.8 us -> 0.67 us
    unnamed x18 -> x0, waiting for transfers between devices: 271 us -> none
    dot_general x17 -> x0, matrix products: 246 us -> none  [the longest x6 104 us: layer(): up = jnp.dot(a, w['w_up'], preferred_element_type=jnp.float32)]
    pallas_call x0 -> x1, Pallas kernels: none -> 211 us  [local(): pl.pallas_call(functools.partial(kernel, (tokens, width, hidden, layers,...]
    squeeze x6 -> x0, waiting for transfers between devices: 136 us -> none  [stack(): h = layer(h, {name: w[number] for name, w in weights.items()})]
    unnamed x3 -> x0, other arithmetic: 55.3 us -> none
    unnamed x21 -> x10, local copies, waits for them, and re-layouts: 26.6 us -> 6.55 us
    reshape x4 -> x0, other arithmetic: 9.68 us -> none  [the longest x1 7.61 us: step(): by_x.reshape(shape)]
  transfers between devices with their start and end apart: 12 -> 0, of which waited for: 10 -> 0; matrix products, arithmetic and copies ran while one was open for 34% -> 0% of each run, Pallas kernels for 0% -> 0%
where the time goes in v1:
time: 220 us; the launch traced here: 219 us
  Pallas kernels  211 us (96%)
  local copies, waits for them, and re-layouts  6.55 us (3%)
    pallas_call x1, Pallas kernels, local(): pl.pallas_call(functools.partial(kernel, (tokens, width, hidden, layers,...  211 us
    unnamed x10, local copies, waits for them, and re-layouts  6.55 us

profile of v1, /device:TPU:96, one launch (start us, length us, event | category | flops | bytes accessed | tf_op | source)
XLA Modules:
  0.0 218.7 jit_solution(10370834241415461317)
XLA Ops:
  0.6 211.5 %stack.1 = (bf16[4096,512]{1,0:T(8,128)(2,1)}, bf16[2,32,1408]{2,1,0:T(8,128)(2,1)}, bf16[2,32,1408]{2,1,0:T(8,128)(2,1)}, bf16[2,88,512]{2,1,0:T(8,128)(2,1)}) custom-call(bf16[4096,512]{1,0:T(8,128)(2,1)} %bitcast.3, bf16[4096,512]{1,0:T(8,128)(2,1)} %bitcast.4, bf16[2,32,1408]{2,1,0:T(8,128)(2,1)} %wg_ref.1, bf16[2,32,1408]{2,1,0:T(8,128)(2,1)} %wu_ref.1, ...), custom_call_target="tpu_custom_call" | custom-call | tf_op jit(solution)/shard_map/stack/pallas_call | solution.py:264
  212.1 0.0 copy-start.2
  212.1 0.0 copy-start.1
  212.1 0.0 copy-start
  212.1 4.5 %copy.13 = bf16[1,4096,512]{2,1,0:T(8,128)(2,1)} copy(bf16[1,4096,512]{2,1,0:T(8,128)(2,1)} %bitcast.5) | data formatting | bytes 8388608
  216.7 0.0 copy-done.2
  216.7 0.7 copy.14
  217.3 0.0 copy-done.1
  217.3 0.7 copy.15
  218.0 0.0 copy-done
  218.0 0.7 copy.16
Async XLA Ops:
  212.1 4.6 %copy-start.2 = (bf16[2,32,1408]{2,1,0:T(8,128)(2,1)S(1)}, bf16[2,32,1408]{2,1,0:T(8,128)(2,1)}, u32[]{:S(2)}) copy-start(bf16[2,32,1408]{2,1,0:T(8,128)(2,1)} %get-tuple-element.17) | copy-start | bytes 540676
  212.1 5.2 %copy-start.1 = (bf16[2,32,1408]{2,1,0:T(8,128)(2,1)S(1)}, bf16[2,32,1408]{2,1,0:T(8,128)(2,1)}, u32[]{:S(2)}) copy-start(bf16[2,32,1408]{2,1,0:T(8,128)(2,1)} %get-tuple-element.18) | copy-start | bytes 540676
  212.1 5.9 %copy-start = (bf16[2,88,512]{2,1,0:T(8,128)(2,1)S(1)}, bf16[2,88,512]{2,1,0:T(8,128)(2,1)}, u32[]{:S(2)}) copy-start(bf16[2,88,512]{2,1,0:T(8,128)(2,1)} %get-tuple-element.19) | copy-start | bytes 540676

commit v2 on v0

v2 whole, which is shorter than its diff:
```python
import functools
import math

import jax
import jax.numpy as jnp
from jax import lax
from jax.experimental import pallas as pl
from jax.experimental.pallas import tpu as pltpu
from jax.sharding import PartitionSpec as P

bf16, f32 = jnp.bfloat16, jnp.float32
MESH = pl.DeviceIdType.MESH
TILE = 512
CHUNK = 256
STEPS = 4
DIMS = ((1, 0), (0, 1), (3, 0), (0, 3))
PART = (0, 1, 0, 1, 2, 3, 2, 3, 0, 1, 2, 3)


def dot(a, b):
    return jnp.dot(a, b, preferred_element_type=f32)


def dot_t(a, b):
    return lax.dot_general(a, b, (((0,), (0,)), ((), ())), preferred_element_type=f32)


def flip(c, bits):
    return (c, c + 1 - 2 * lax.rem(c, 2), lax.rem(c + 2, 4), 3 - c)[bits]


def mask_of(part, slot):
    x = y = 0
    for bit in range(STEPS):
        if slot >> bit & 1:
            dx, dy = DIMS[(part + STEPS - 1 - bit) % 4]
            x, y = x ^ dx, y ^ dy
    return x, y


def kernel(sizes, x_hbm, dy_hbm, wg_ref, wu_ref, wd_ref, dx_hbm, og_ref, ou_ref, od_ref, p_hbm, dgu_hbm, *scratch):
    (x_s, h_s, dy_s, wgu, wd0, wgut, wdt, acc_gu, acc_d, p_s, dgu_s, *rest) = scratch
    slots = (rest[:12], rest[12:24])
    send_sem, recv_sem, hand_send, hand_recv, credit, copy_sem, out_sem, p_sem, dgu_sem = rest[24:]
    tokens, width, hidden, share_gu, share_d = sizes
    me, rep = lax.axis_index("dp"), lax.axis_index("rep")
    mx, my = lax.div(me, 4), lax.rem(me, 4)
    core = lax.rem(rep, 2)
    tiles = tokens // TILE

    def device(mask):
        return flip(mx, mask[0]) * 4 + flip(my, mask[1])

    def to(dim):
        return {"dp": device(DIMS[dim % 4])}

    partner = {"rep": rep + 1 - 2 * core}
    pieces = pieces_of(hidden)
    cols = pieces + [(hidden + lo, hidden + hi) for lo, hi in pieces] + [(width * q // 4, width * (q + 1) // 4) for q in range(4)]
    GU, D = range(8), range(8, 12)
    half = pieces[2][0]
    FIRST, SECOND = (0, 1, 4, 5), (2, 3, 6, 7)
    keeper = (0, 0, 0, 0, 1, 1, 1, 1, 0, 0, 1, 1)

    copies = [pltpu.make_async_copy(x_hbm, x_s, copy_sem.at[0]), pltpu.make_async_copy(dy_hbm, dy_s, copy_sem.at[1])]
    for copy in copies:
        copy.start()

    barrier = pltpu.get_barrier_semaphore()
    for peer in [to(dim) for dim in range(4)] + [partner]:
        pl.semaphore_signal(barrier, inc=1, device_id=peer, device_id_type=MESH)

    def rows_of(a, slot):
        share = share_gu if a < 8 else share_d
        return pl.ds(pl.multiple_of(device(mask_of(PART[a], slot)) * share, 8), share)

    def own_blocks(layer):
        for a, (lo, hi) in enumerate(cols):
            if a < 4:
                slots[layer][a][0] = wg_ref[layer, :, lo:hi]
            elif a < 8:
                slots[layer][a][0] = wu_ref[layer, :, lo - hidden:hi - hidden]
            else:
                slots[layer][a][0] = wd_ref[layer, :, lo:hi]

    def gather_copy(layer, step, a):
        n = 2**step
        return pltpu.make_async_remote_copy(
            src_ref=slots[layer][a].at[pl.ds(0, n)], dst_ref=slots[layer][a].at[pl.ds(n, n)],
            send_sem=send_sem.at[layer, a, step], recv_sem=recv_sem.at[layer, a, step],
            device_id=to(PART[a] + STEPS - 1 - step), device_id_type=MESH)

    def hand_copy(layer, step, a):
        there = slots[layer][a].at[pl.ds(2**step, 2**step)]
        return pltpu.make_async_remote_copy(
            src_ref=there, dst_ref=there, send_sem=hand_send.at[layer, a, step], recv_sem=hand_recv.at[layer, a, step],
            device_id=partner, device_id_type=MESH)

    def by_core(arrays, act):
        for side in range(2):
            @pl.when(core == side)
            def _():
                act([a for a in arrays if keeper[a] == side], [a for a in arrays if keeper[a] != side])

    def gather_step(layer, step, arrays, then=None):
        def act(mine, _):
            for a in mine:
                if step > 0:
                    gather_copy(layer, step - 1, a).wait()
                if step < STEPS:
                    gather_copy(layer, step, a).start()
                if step > 0:
                    hand_copy(layer, step - 1, a).start()
        by_core(arrays, act)

    def gather_end(layer, arrays):
        def act(mine, others):
            for step in range(STEPS):
                for a in others:
                    hand_copy(layer, step, a).wait_recv()
                for a in mine:
                    hand_copy(layer, step, a).wait_send()
        by_core(arrays, act)

    def install(layer, arrays):
        for r in range(16):
            for a in arrays:
                lo, hi = cols[a]
                if a < 8:
                    wgu[layer, rows_of(a, r), lo:hi] = slots[layer][a][r]
                else:
                    acc_d[layer, rows_of(a, r), lo:hi] = slots[layer][a][r].astype(f32)

    def scatter_copy(layer, step, a):
        n = 2 ** (STEPS - 1 - step)
        return pltpu.make_async_remote_copy(
            src_ref=slots[1][a].at[pl.ds(n, n)], dst_ref=slots[0][a].at[pl.ds(n, n)],
            send_sem=send_sem.at[2 + layer, a, step], recv_sem=recv_sem.at[2 + layer, a, step],
            device_id=to(PART[a] + step), device_id_type=MESH)

    def scatter_start(layer, step, arrays):
        for a in arrays:
            if layer == 0:
                pl.semaphore_wait(credit.at[a, step], 1)
            scatter_copy(layer, step, a).start()

    def scatter_fill(layer, arrays):
        for a in arrays:
            lo, hi = cols[a]
            acc = acc_gu if a < 8 else acc_d
            for r in range(8, 16):
                slots[1][a][r] = acc[layer, rows_of(a, r), lo:hi].astype(bf16)
        scatter_start(layer, 0, arrays)

    def scatter_add(layer, step, arrays):
        n = 2 ** (STEPS - 1 - step)
        for a in arrays:
            lo, hi = cols[a]
            scatter_copy(layer, step, a).wait()
            acc = acc_gu if a < 8 else acc_d
            for r in reversed(range(n)):
                total = acc[layer, rows_of(a, r), lo:hi] + slots[0][a][n + r].astype(f32)
                if n == 1:
                    if a < 4:
                        og_ref[layer, :, lo:hi] = total.astype(bf16)
                    elif a < 8:
                        ou_ref[layer, :, lo - hidden:hi - hidden] = total.astype(bf16)
                    else:
                        od_ref[layer, :, lo:hi] = total.astype(bf16)
                elif r >= n // 2:
                    slots[1][a][r] = total.astype(bf16)
                else:
                    acc[layer, rows_of(a, r), lo:hi] = total
            if layer == 1:
                pl.semaphore_signal(credit.at[a, step], inc=1, device_id=to(PART[a] + step), device_id_type=MESH)
        if step < STEPS - 1:
            scatter_start(layer, step + 1, arrays)

    def chunks_of(lo, hi):
        return [(at, min(at + CHUNK, hi)) for at in range(lo, hi, CHUNK)]

    def normed(ref, rows):
        wide = ref[rows, :].astype(f32)
        scale = lax.rsqrt(jnp.mean(wide * wide, -1, keepdims=True) + 1e-6)
        return wide, scale, (wide * scale).astype(bf16)

    def at_tile(i):
        return pl.ds(pl.multiple_of(i * TILE, TILE), TILE)

    def loop(events, body):
        def step(i, _):
            for when, actions in events.items():
                @pl.when(i == when)
                def _():
                    for act, *args in actions:
                        act(*args)
            body(i)
            return 0
        lax.fori_loop(0, tiles, step, 0)

    def transposes(layer, down):
        for lo in range(0, 2 * hidden, CHUNK):
            wgut[lo:lo + CHUNK, :] = wgu[layer, :, lo:lo + CHUNK].T
        for lo, hi in chunks_of(0, hidden):
            wdt[:, lo:hi] = down[lo:hi, :].T.astype(bf16)

    def inner(layer, a, dy, span, dgu_ref, p_ref=None):
        for lo, hi in chunks_of(*span):
            g, u = dot(a, wgu[layer, :, lo:hi]), dot(a, wgu[layer, :, hidden + lo:hidden + hi])
            dq = dot(dy, wdt[:, lo:hi]).astype(bf16).astype(f32)
            sig = 0.5 * jnp.tanh(0.5 * g) + 0.5
            s = g * sig
            if p_ref is not None:
                p_ref[:, lo:hi] = (s * u).astype(bf16)
            dgu_ref[:, hidden + lo:hidden + hi] = (dq * s).astype(bf16)
            dgu_ref[:, lo:hi] = (dq * u * (sig + s * (1 - sig))).astype(bf16)

    def outer(wide, scale, dy, dgu_ref):
        da = dot(dgu_ref[...], wgut[...]).astype(bf16).astype(f32)
        mean = jnp.mean(da * wide, -1, keepdims=True)
        return dy + (da * scale - wide * (mean * scale * scale * scale)).astype(bf16)

    own_blocks(0)
    own_blocks(1)
    pl.semaphore_wait(barrier, 5)
    gather_step(0, 0, GU)
    gather_step(0, 0, D)
    gather_step(0, 1, GU)
    gather_step(0, 1, D)
    gather_step(0, 2, GU)
    gather_step(0, 2, D)
    gather_step(0, 3, GU)
    gather_step(0, 3, D)
    gather_step(1, 0, range(12))
    acc_gu[...] = jnp.zeros_like(acc_gu)
    gather_step(0, 4, GU)
    gather_end(0, GU)
    install(0, GU)
    for copy in copies:
        copy.wait()

    def p_copy(i, out):
        there, here = p_hbm.at[at_tile(i)], p_s.at[lax.rem(i, 2)]
        return pltpu.make_async_copy(*((here, there) if out else (there, here)), p_sem.at[lax.rem(i, 2)])

    def forward(i):
        rows = at_tile(i)
        slot = lax.rem(i, 2)
        _, _, a = normed(x_s, rows)

        @pl.when(i >= 2)
        def _():
            p_copy(i - 2, True).wait()
        for lo, hi in chunks_of(0, hidden):
            g, u = dot(a, wgu[0, :, lo:hi]), dot(a, wgu[0, :, hidden + lo:hidden + hi])
            p_s[slot, :, lo:hi] = (g * (0.5 * jnp.tanh(0.5 * g) + 0.5) * u).astype(bf16)
        p_copy(i, True).start()

        @pl.when(i == 0)
        def _():
            gather_step(0, 4, D)
            gather_end(0, D)
            install(0, D)
            wd0[...] = acc_d[0].astype(bf16)
        h_s[rows, :] = x_s[rows, :] + dot(p_s[slot], wd0[...]).astype(bf16)

    every = range(12)
    loop({1: [(gather_step, 1, 1, every)], 2: [(gather_step, 1, 2, every)], 4: [(gather_step, 1, 3, every)], 7: [(gather_step, 1, 4, every)]}, forward)
    p_copy(tiles - 2, True).wait()
    p_copy(tiles - 1, True).wait()
    gather_end(1, every)
    install(1, every)
    transposes(1, acc_d.at[1])
    acc_d[...] = jnp.zeros_like(acc_d)

    def last(i):
        rows = at_tile(i)
        wide, scale, a = normed(h_s, rows)
        dy = dy_s[rows, :]
        inner(1, a, dy, (0, hidden), dgu_s.at[0], p_s.at[0])
        acc_d[1] += dot_t(p_s[0], dy)
        acc_gu[1] += dot_t(a, dgu_s[0])
        h_s[rows, :] = outer(wide, scale, dy, dgu_s.at[0])

    loop({}, last)
    p_copy(0, False).start()
    scatter_fill(1, every)
    transposes(0, wd0)

    def down(i):
        slot = lax.rem(i, 2)

        @pl.when(i < tiles - 1)
        def _():
            p_copy(i + 1, False).start()
        p_copy(i, False).wait()
        acc_d[0] += dot_t(p_s[slot], h_s[at_tile(i), :])

    def dgu_copies(i, span, out):
        slot = lax.rem(i, 2)
        found = []
        for side in range(2):
            place = pl.ds(side * hidden + span[0], span[1] - span[0])
            there, here = dgu_hbm.at[at_tile(i), place], dgu_s.at[slot, :, place]
            found.append(pltpu.make_async_copy(*((here, there) if out else (there, here)), dgu_sem.at[slot, side]))
        return found

    def gate_up(i, span):
        slot = lax.rem(i, 2)
        rows = at_tile(i)
        _, _, a = normed(x_s, rows)

        @pl.when(i >= 2)
        def _():
            for copy in dgu_copies(i - 2, span, True):
                copy.wait()
        inner(0, a, h_s[rows, :], span, dgu_s.at[slot])
        for copy in dgu_copies(i, span, True):
            copy.start()
        for side in range(2):
            lo, hi = (side * hidden + at for at in span)
            acc_gu[0, :, lo:hi] += dot_t(a, dgu_s[slot, :, lo:hi])

    def drain(span):
        for i in range(tiles - 2, tiles):
            for copy in dgu_copies(i, span, True):
                copy.wait()

    def out_copy(i):
        return pltpu.make_async_copy(x_s.at[at_tile(i)], dx_hbm.at[at_tile(i)], out_sem.at[i])

    def back(i):
        slot = lax.rem(i, 2)
        whole = (0, hidden)
        rows = at_tile(i)

        @pl.when(i < tiles - 1)
        def _():
            for copy in dgu_copies(i + 1, whole, False):
                copy.start()
        for copy in dgu_copies(i, whole, False):
            copy.wait()
        wide, scale, _ = normed(x_s, rows)
        x_s[rows, :] = outer(wide, scale, h_s[rows, :], dgu_s.at[slot])
        out_copy(i).start()

    loop({}, down)
    loop({2: [(scatter_add, 1, 0, every), (scatter_fill, 0, D)], 4: [(scatter_add, 1, 1, every)], 5: [(scatter_add, 0, 0, D), (scatter_add, 1, 2, every)],
          6: [(scatter_add, 0, 1, D)], 7: [(scatter_add, 1, 3, every), (scatter_add, 0, 2, D)]}, lambda i: gate_up(i, (0, half)))
    drain((0, half))
    scatter_fill(0, FIRST)
    loop({1: [(scatter_add, 0, 3, D)], 3: [(scatter_add, 0, 0, FIRST)], 5: [(scatter_add, 0, 1, FIRST)], 7: [(scatter_add, 0, 2, FIRST)]},
         lambda i: gate_up(i, (half, hidden)))
    drain((half, hidden))
    for copy in dgu_copies(0, (0, hidden), False):
        copy.start()
    scatter_fill(0, SECOND)
    loop({0: [(scatter_add, 0, 3, FIRST)], 3: [(scatter_add, 0, 0, SECOND)], 5: [(scatter_add, 0, 1, SECOND)], 7: [(scatter_add, 0, 2, SECOND)]}, back)
    scatter_add(0, 3, SECOND)
    for i in range(tiles):
        out_copy(i).wait()


def pieces_of(hidden):
    lanes = hidden // 128
    cuts = [128 * -(-lanes * q // 4) for q in range(5)]
    return list(zip(cuts, cuts[1:]))


def solution(mesh):
    group = mesh.shape["dp"]
    side = math.isqrt(group)
    assert side * side == group == 2**STEPS

    def local(x, dy, w_gate, w_up, w_down):
        _, tokens, width = x.shape
        layers, share_gu, hidden = w_gate.shape
        share_d = w_down.shape[1]
        parts = [pltpu.VMEM((group, share_gu, hi - lo), bf16) for lo, hi in pieces_of(hidden) * 2]
        parts += [pltpu.VMEM((group, share_d, width // 4), bf16)] * 4
        any_, vmem = pl.BlockSpec(memory_space=pl.ANY), pl.BlockSpec(memory_space=pltpu.VMEM)
        shapes = ((tokens, width), w_gate.shape, w_up.shape, w_down.shape, (tokens, hidden), (tokens, 2 * hidden))
        dma, tiles = pltpu.SemaphoreType.DMA, tokens // TILE
        out = pl.pallas_call(
            functools.partial(kernel, (tokens, width, hidden, share_gu, share_d)),
            out_shape=[jax.ShapeDtypeStruct(s, bf16) for s in shapes],
            in_specs=[any_, any_, vmem, vmem, vmem],
            out_specs=[any_, vmem, vmem, vmem, any_, any_],
            scratch_shapes=[pltpu.VMEM((tokens, width), bf16)] * 3 + [
                pltpu.VMEM((layers, width, 2 * hidden), bf16),
                pltpu.VMEM((hidden, width), bf16),
                pltpu.VMEM((2 * hidden, width), bf16),
                pltpu.VMEM((width, hidden), bf16),
                pltpu.VMEM((layers, width, 2 * hidden), f32),
                pltpu.VMEM((layers, hidden, width), f32),
                pltpu.VMEM((2, TILE, hidden), bf16),
                pltpu.VMEM((2, TILE, 2 * hidden), bf16),
            ] + parts * 2 + [
                dma((4, 12, STEPS)), dma((4, 12, STEPS)), dma((2, 12, STEPS)), dma((2, 12, STEPS)),
                pltpu.SemaphoreType.REGULAR((12, STEPS)), dma((2,)), dma((tiles,)), dma((2,)), dma((2, 2)),
            ],
            compiler_params=pltpu.CompilerParams(collective_id=0, has_side_effects=True, vmem_limit_bytes=67043328),
            name="stack",
        )(x[0], dy[0], w_gate, w_up, w_down)
        return (out[0][None], *out[1:4])

    tokens_spec = P(("rep", "dp"), None, None)
    weight_spec, grad_spec = P(None, "dp", None), P("rep", "dp", None)
    return jax.shard_map(local, mesh=mesh, in_specs=(tokens_spec, tokens_spec) + (weight_spec,) * 3,
                         out_specs=(tokens_spec,) + (grad_spec,) * 3, check_vma=False)
```

time: 790 us -> 209 us (0.26); the launches traced: 781 us -> 209 us
  waiting for transfers between devices: 407 us -> 0 us
  matrix products: 246 us -> 0 us
  Pallas kernels: 0 us -> 202 us
  other arithmetic: 80.4 us -> 0 us
  local copies, waits for them, and re-layouts: 31.5 us -> 6.55 us
  between operations: 14.8 us -> 0.67 us
    unnamed x18 -> x0, waiting for transfers between devices: 271 us -> none
    dot_general x17 -> x0, matrix products: 246 us -> none  [the longest x6 104 us: layer(): up = jnp.dot(a, w['w_up'], preferred_element_type=jnp.float32)]
    pallas_call x0 -> x1, Pallas kernels: none -> 202 us  [local(): pl.pallas_call(functools.partial(kernel, (tokens, width, hidden, share_gu...]
    squeeze x6 -> x0, waiting for transfers between devices: 136 us -> none  [stack(): h = layer(h, {name: w[number] for name, w in weights.items()})]
    unnamed x3 -> x0, other arithmetic: 55.3 us -> none
    unnamed x21 -> x10, local copies, waits for them, and re-layouts: 26.6 us -> 6.55 us
    reshape x4 -> x0, other arithmetic: 9.68 us -> none  [the longest x1 7.61 us: step(): by_x.reshape(shape)]
  transfers between devices with their start and end apart: 12 -> 0, of which waited for: 10 -> 0; matrix products, arithmetic and copies ran while one was open for 34% -> 0% of each run, Pallas kernels for 0% -> 0%
where the time goes in v2:
time: 209 us
  Pallas kernels  202 us (97%)
  local copies, waits for them, and re-layouts  6.55 us (3%)
    pallas_call x1, Pallas kernels, local(): pl.pallas_call(functools.partial(kernel, (tokens, width, hidden, share_gu...  202 us
    unnamed x10, local copies, waits for them, and re-layouts  6.55 us

profile of v2, /device:TPU:96, one launch (start us, length us, event | category | flops | bytes accessed | tf_op | source)
XLA Modules:
  0.0 208.9 jit_solution(4861659531418238136)
XLA Ops:
  0.6 201.7 %stack.1 = (bf16[4096,512]{1,0:T(8,128)(2,1)}, bf16[2,32,1408]{2,1,0:T(8,128)(2,1)}, bf16[2,32,1408]{2,1,0:T(8,128)(2,1)}, bf16[2,88,512]{2,1,0:T(8,128)(2,1)}, ...) custom-call(bf16[4096,512]{1,0:T(8,128)(2,1)} %bitcast.3, bf16[4096,512]{1,0:T(8,128)(2,1)} %bitcast.4, ...), custom_call_target="tpu_custom_call" | custom-call | tf_op jit(solution)/shard_map/stack/pallas_call | solution.py:384
  202.4 0.0 copy-start.2
  202.4 0.0 copy-start.1
  202.4 0.0 copy-start
  202.4 4.5 %copy.13 = bf16[1,4096,512]{2,1,0:T(8,128)(2,1)} copy(bf16[1,4096,512]{2,1,0:T(8,128)(2,1)} %bitcast.5) | data formatting | bytes 8388608
  206.9 0.0 copy-done.2
  206.9 0.7 copy.14
  207.6 0.0 copy-done.1
  207.6 0.7 copy.15
  208.3 0.0 copy-done
  208.3 0.7 copy.16
Async XLA Ops:
  202.4 4.6 %copy-start.2 = (bf16[2,32,1408]{2,1,0:T(8,128)(2,1)S(1)}, bf16[2,32,1408]{2,1,0:T(8,128)(2,1)}, u32[]{:S(2)}) copy-start(bf16[2,32,1408]{2,1,0:T(8,128)(2,1)} %get-tuple-element.17) | copy-start | bytes 540676
  202.4 5.2 %copy-start.1 = (bf16[2,32,1408]{2,1,0:T(8,128)(2,1)S(1)}, bf16[2,32,1408]{2,1,0:T(8,128)(2,1)}, u32[]{:S(2)}) copy-start(bf16[2,32,1408]{2,1,0:T(8,128)(2,1)} %get-tuple-element.18) | copy-start | bytes 540676
  202.4 5.9 %copy-start = (bf16[2,88,512]{2,1,0:T(8,128)(2,1)S(1)}, bf16[2,88,512]{2,1,0:T(8,128)(2,1)}, u32[]{:S(2)}) copy-start(bf16[2,88,512]{2,1,0:T(8,128)(2,1)} %get-tuple-element.19) | copy-start | bytes 540676

commit v3 on v2

v3 whole, which is shorter than its diff:
```python
import functools
import math

import jax
import jax.numpy as jnp
from jax import lax
from jax.experimental import pallas as pl
from jax.experimental.pallas import tpu as pltpu
from jax.sharding import PartitionSpec as P

bf16, f32 = jnp.bfloat16, jnp.float32
MESH = pl.DeviceIdType.MESH
TILE = 512
CHUNK = 256
STEPS = 4
VMEM_LIMIT = 67043328
DIMS = ((1, 0), (0, 1), (3, 0), (0, 3))
PART = (0, 1, 0, 1, 2, 3, 2, 3, 0, 1, 2, 3)


def dot(a, b):
    return jnp.dot(a, b, preferred_element_type=f32)


def dot_t(a, b):
    return lax.dot_general(a, b, (((0,), (0,)), ((), ())), preferred_element_type=f32)


def flip(c, bits):
    return (c, c + 1 - 2 * lax.rem(c, 2), lax.rem(c + 2, 4), 3 - c)[bits]


def mask_of(part, slot):
    x = y = 0
    for bit in range(STEPS):
        if slot >> bit & 1:
            dx, dy = DIMS[(part + STEPS - 1 - bit) % 4]
            x, y = x ^ dx, y ^ dy
    return x, y


def kernel(sizes, x_hbm, dy_hbm, wg_hbm, wu_hbm, wd_hbm, h_s, og_hbm, ou_hbm, od_hbm, p_hbm, dgu_hbm, a_hbm, gu_hbm, *scratch):
    (in_s, gu_s, wgu, wgut, wdt, acc_gu, acc_d, p_s, dgu_s, *rest) = scratch
    slots = (rest[:12], rest[12:24])
    send_sem, recv_sem, hand_send, hand_recv, credit, own_sem, in_sem, a_sem, p_sem, dgu_sem, gu_sem = rest[24:]
    tokens, width, hidden, share_gu, share_d = sizes
    a_s = dgu_s.at[:, :, :width]
    wd0 = [(lo, min(lo + TILE, hidden), dgu_s.at[1, :min(TILE, hidden - lo), pl.ds((1 + lo // TILE) * width, width)]) for lo in range(0, hidden, TILE)]
    me, rep = lax.axis_index("dp"), lax.axis_index("rep")
    mx, my = lax.div(me, 4), lax.rem(me, 4)
    core = lax.rem(rep, 2)
    tiles = tokens // TILE

    def device(mask):
        return flip(mx, mask[0]) * 4 + flip(my, mask[1])

    def to(dim):
        return {"dp": device(DIMS[dim % 4])}

    partner = {"rep": rep + 1 - 2 * core}
    pieces = pieces_of(hidden)
    cols = pieces + [(hidden + lo, hidden + hi) for lo, hi in pieces] + [(width * q // 4, width * (q + 1) // 4) for q in range(4)]
    GU, D = range(8), range(8, 12)
    half = pieces[2][0]
    FIRST, SECOND = (0, 1, 4, 5), (2, 3, 6, 7)
    keeper = (0, 0, 0, 0, 1, 1, 1, 1, 0, 0, 1, 1)

    def in_copy(source, i):
        return pltpu.make_async_copy(source.at[at_tile(i)], in_s.at[lax.rem(i, 2)], in_sem.at[lax.rem(i, 2)])

    def streamed(source, following, i):
        @pl.when(i < tiles - 1)
        def _():
            in_copy(source, i + 1).start()
        if following is not None:
            @pl.when(i == tiles - 1)
            def _():
                in_copy(following, 0).start()
        in_copy(source, i).wait()
        return in_s[lax.rem(i, 2)]

    def at_tile(i):
        if isinstance(i, int):
            return pl.ds(i * TILE, TILE)
        return pl.ds(pl.multiple_of(i * TILE, TILE), TILE)

    def start(copies):
        for copy in copies:
            copy.start()

    def wait(copies):
        for copy in copies:
            copy.wait()

    def rows_of(a, slot):
        share = share_gu if a < 8 else share_d
        return pl.ds(pl.multiple_of(device(mask_of(PART[a], slot)) * share, 8), share)

    def own(layer, a, g, u, d):
        lo, hi = cols[a]
        return g.at[layer, :, lo:hi] if a < 4 else u.at[layer, :, lo - hidden:hi - hidden] if a < 8 else d.at[layer, :, lo:hi]

    def own_copy(layer, a):
        return pltpu.make_async_copy(own(layer, a, wg_hbm, wu_hbm, wd_hbm), slots[layer][a].at[0], own_sem.at[layer, a])

    def result_copy(layer, a):
        return pltpu.make_async_copy(slots[1][a].at[0], own(layer, a, og_hbm, ou_hbm, od_hbm), own_sem.at[layer, a])

    def gather_copy(layer, step, a):
        n = 2**step
        return pltpu.make_async_remote_copy(
            src_ref=slots[layer][a].at[pl.ds(0, n)], dst_ref=slots[layer][a].at[pl.ds(n, n)],
            send_sem=send_sem.at[layer, a, step], recv_sem=recv_sem.at[layer, a, step],
            device_id=to(PART[a] + STEPS - 1 - step), device_id_type=MESH)

    def hand_copy(layer, step, a):
        there = slots[layer][a].at[pl.ds(2**step, 2**step)]
        return pltpu.make_async_remote_copy(
            src_ref=there, dst_ref=there, send_sem=hand_send.at[layer, a, step], recv_sem=hand_recv.at[layer, a, step],
            device_id=partner, device_id_type=MESH)

    def by_core(arrays, act):
        for side in range(2):
            @pl.when(core == side)
            def _():
                act([a for a in arrays if keeper[a] == side], [a for a in arrays if keeper[a] != side])

    def gather_step(layer, step, arrays, then=None):
        def act(mine, _):
            for a in mine:
                if step > 0:
                    gather_copy(layer, step - 1, a).wait()
                if step < STEPS:
                    gather_copy(layer, step, a).start()
                if step > 0:
                    hand_copy(layer, step - 1, a).start()
        by_core(arrays, act)

    def gather_end(layer, arrays):
        def act(mine, others):
            for step in range(STEPS):
                for a in others:
                    hand_copy(layer, step, a).wait_recv()
                for a in mine:
                    hand_copy(layer, step, a).wait_send()
        by_core(arrays, act)

    def install(layer, arrays):
        for r in range(16):
            for a in arrays:
                lo, hi = cols[a]
                if a < 8:
                    wgu[layer, rows_of(a, r), lo:hi] = slots[layer][a][r]
                else:
                    acc_d[layer, rows_of(a, r), lo:hi] = slots[layer][a][r].astype(f32)

    def scatter_copy(layer, step, a):
        n = 2 ** (STEPS - 1 - step)
        return pltpu.make_async_remote_copy(
            src_ref=slots[1][a].at[pl.ds(n, n)], dst_ref=slots[0][a].at[pl.ds(n, n)],
            send_sem=send_sem.at[2 + layer, a, step], recv_sem=recv_sem.at[2 + layer, a, step],
            device_id=to(PART[a] + step), device_id_type=MESH)

    def scatter_start(layer, step, arrays):
        for a in arrays:
            if layer == 0:
                pl.semaphore_wait(credit.at[a, step], 1)
            scatter_copy(layer, step, a).start()

    def scatter_fill(layer, arrays):
        for a in arrays:
            lo, hi = cols[a]
            acc = acc_gu if a < 8 else acc_d
            for r in range(8, 16):
                slots[1][a][r] = acc[layer, rows_of(a, r), lo:hi].astype(bf16)
        scatter_start(layer, 0, arrays)

    def scatter_add(layer, step, arrays):
        n = 2 ** (STEPS - 1 - step)
        for a in arrays:
            lo, hi = cols[a]
            scatter_copy(layer, step, a).wait()
            acc = acc_gu if a < 8 else acc_d
            for r in reversed(range(n)):
                total = acc[layer, rows_of(a, r), lo:hi] + slots[0][a][n + r].astype(f32)
                if n == 1:
                    if layer == 0:
                        result_copy(1, a).wait()
                    slots[1][a][0] = total.astype(bf16)
                    result_copy(layer, a).start()
                elif r >= n // 2:
                    slots[1][a][r] = total.astype(bf16)
                else:
                    acc[layer, rows_of(a, r), lo:hi] = total
            if layer == 1:
                pl.semaphore_signal(credit.at[a, step], inc=1, device_id=to(PART[a] + step), device_id_type=MESH)
        if step < STEPS - 1:
            scatter_start(layer, step + 1, arrays)

    def chunks_of(lo, hi):
        return [(at, min(at + CHUNK, hi)) for at in range(lo, hi, CHUNK)]

    def normed(h):
        wide = h.astype(f32)
        scale = lax.rsqrt(jnp.mean(wide * wide, -1, keepdims=True) + 1e-6)
        return wide, scale, (wide * scale).astype(bf16)

    def loop(events, body, n=tiles):
        def step(i, _):
            for when, actions in events.items():
                @pl.when(i == when)
                def _():
                    for act, *args in actions:
                        act(*args)
            body(i)
            return 0
        lax.fori_loop(0, n, step, 0)

    def transposes(layer, down):
        for lo in range(0, 2 * hidden, CHUNK):
            wgut[lo:lo + CHUNK, :] = wgu[layer, :, lo:lo + CHUNK].T
        for lo, hi, block in down:
            wdt[:, lo:hi] = block[...].T.astype(bf16)

    def inner(g, u, dq):
        dq = dq.astype(bf16).astype(f32)
        sig = 0.5 * jnp.tanh(0.5 * g) + 0.5
        s = g * sig
        return (s * u).astype(bf16), (dq * u * (sig + s * (1 - sig))).astype(bf16), (dq * s).astype(bf16)

    def outer(wide, scale, dy, da):
        da = da.astype(bf16).astype(f32)
        mean = jnp.mean(da * wide, -1, keepdims=True)
        return dy + (da * scale - wide * (mean * scale * scale * scale)).astype(bf16)

    every = range(12)
    for layer in range(2):
        start([own_copy(layer, a) for a in every])
    in_copy(x_hbm, 0).start()
    barrier = pltpu.get_barrier_semaphore()
    for peer in [to(dim) for dim in range(4)] + [partner]:
        pl.semaphore_signal(barrier, inc=1, device_id=peer, device_id_type=MESH)
    wait([own_copy(0, a) for a in every])
    pl.semaphore_wait(barrier, 5)
    gather_step(0, 0, GU)
    gather_step(0, 0, D)
    gather_step(0, 1, GU)
    gather_step(0, 1, D)
    gather_step(0, 2, GU)
    gather_step(0, 2, D)
    gather_step(0, 3, GU)
    gather_step(0, 3, D)
    wait([own_copy(1, a) for a in every])
    gather_step(1, 0, every)
    in_copy(x_hbm, 0).wait()
    a_s[0] = normed(in_s[0])[2]
    gather_step(0, 4, GU)
    gather_end(0, GU)
    install(0, GU)

    def p_out(i):
        return pltpu.make_async_copy(p_s.at[lax.rem(i, 2)], p_hbm.at[at_tile(i)], p_sem.at[lax.rem(i, 2)])

    def gu_out(i):
        return pltpu.make_async_copy(acc_gu.at[lax.rem(i, 2)], gu_hbm.at[at_tile(i)], gu_sem.at[lax.rem(i, 2), 0])

    def a_out(i):
        return pltpu.make_async_copy(a_s.at[lax.rem(i, 2)], a_hbm.at[at_tile(i)], a_sem.at[lax.rem(i, 2)])

    def next_x(i):
        slot = lax.rem(i + 1, 2)
        return pltpu.make_async_copy(x_hbm.at[at_tile(jnp.minimum(i + 1, tiles - 1))], in_s.at[slot], in_sem.at[slot])

    def forward(i):
        slot = lax.rem(i, 2)
        next_x(i).start()
        a_out(i).start()

        @pl.when(i >= 1)
        def _():
            a_out(i - 1).wait()

        @pl.when(i >= 2)
        def _():
            p_out(i - 2).wait()
            gu_out(i - 2).wait()
        a = a_s[slot]
        for lo, hi in chunks_of(0, hidden):
            g, u = dot(a, wgu[0, :, lo:hi]), dot(a, wgu[0, :, hidden + lo:hidden + hi])
            acc_gu[slot, :, lo:hi] = g
            acc_gu[slot, :, hidden + lo:hidden + hi] = u
            p_s[slot, :, lo:hi] = (g * (0.5 * jnp.tanh(0.5 * g) + 0.5) * u).astype(bf16)
        p_out(i).start()
        gu_out(i).start()

        @pl.when(i == 0)
        def _():
            gather_step(0, 4, D)
            gather_end(0, D)
            install(0, D)
            for lo, hi, block in wd0:
                block[...] = acc_d[0, lo:hi].astype(bf16)
        next_x(i).wait()
        down = sum(dot(p_s[slot, :, lo:hi], block[...]) for lo, hi, block in wd0).astype(bf16)
        a_s[1 - slot] = normed(in_s[1 - slot])[2]
        h_s[at_tile(i), :] = in_s[slot] + down

    loop({1: [(gather_step, 1, 1, every)], 2: [(gather_step, 1, 2, every)], 4: [(gather_step, 1, 3, every)], 7: [(gather_step, 1, 4, every)]}, forward)
    a_out(tiles - 1).wait()
    in_copy(dy_hbm, 0).start()
    gather_end(1, every)
    install(1, every)
    transposes(1, [(lo, hi, acc_d.at[1, lo:hi]) for lo, hi in chunks_of(0, hidden)])
    acc_d[...] = jnp.zeros_like(acc_d)
    for i in (tiles - 2, tiles - 1):
        p_out(i).wait()
        gu_out(i).wait()
    acc_gu[...] = jnp.zeros_like(acc_gu)

    def p_in(i):
        return pltpu.make_async_copy(p_hbm.at[at_tile(i)], p_s.at[1], p_sem.at[0])

    def last(i):
        rows = at_tile(i)
        wide, scale, a = normed(h_s[rows, :])
        dy = streamed(dy_hbm, a_hbm, i)
        for lo, hi in chunks_of(0, hidden):
            g, u = dot(a, wgu[1, :, lo:hi]), dot(a, wgu[1, :, hidden + lo:hidden + hi])
            p_s[0, :, lo:hi], dgu_s[0, :, lo:hi], dgu_s[0, :, hidden + lo:hidden + hi] = inner(g, u, dot(dy, wdt[:, lo:hi]))
        dh = outer(wide, scale, dy, dot(dgu_s[0], wgut[...]))
        h_s[rows, :] = dh
        acc_d[1] += dot_t(p_s[0], dy)
        acc_gu[1] += dot_t(a, dgu_s[0])
        p_in(i).wait()
        acc_d[0] += dot_t(p_s[1], dh)

        @pl.when(i < tiles - 1)
        def _():
            p_in(i + 1).start()

    p_in(0).start()
    loop({}, last)
    scatter_fill(1, every)
    transposes(0, [(lo, min(lo + CHUNK, hi), block.at[lo - begin:min(lo + CHUNK, hi) - begin]) for begin, hi, block in wd0 for lo in range(begin, hi, CHUNK)])

    def dgu_copies(i, span, out):
        slot = lax.rem(i, 2)
        found = []
        for side in range(2):
            place = pl.ds(side * hidden + span[0], span[1] - span[0])
            there, here = dgu_hbm.at[at_tile(i), place], dgu_s.at[slot, :, place]
            found.append(pltpu.make_async_copy(*((here, there) if out else (there, here)), dgu_sem.at[slot, side]))
        return found

    def gu_in(i, span):
        slot, n = lax.rem(i, 2), span[1] - span[0]
        return [pltpu.make_async_copy(gu_hbm.at[at_tile(i), pl.ds(side * hidden + span[0], n)], gu_s.at[slot, :, pl.ds(side * half, n)],
                                      gu_sem.at[slot, side]) for side in range(2)]

    def gate_up(i, span, following):
        slot = lax.rem(i, 2)
        dy = h_s[at_tile(i), :]
        a = streamed(a_hbm, following, i)

        @pl.when(i < tiles - 1)
        def _():
            start(gu_in(i + 1, span))

        @pl.when(i >= 2)
        def _():
            wait(dgu_copies(i - 2, span, True))
        wait(gu_in(i, span))
        for lo, hi in chunks_of(*span):
            here = [slice(at + lo - span[0], at + hi - span[0]) for at in (0, half)]
            _, dgu_s[slot, :, lo:hi], dgu_s[slot, :, hidden + lo:hidden + hi] = inner(gu_s[slot, :, here[0]], gu_s[slot, :, here[1]], dot(dy, wdt[:, lo:hi]))
        start(dgu_copies(i, span, True))
        for side in range(2):
            lo, hi = (side * hidden + at for at in span)
            acc_gu[0, :, lo:hi] += dot_t(a, dgu_s[slot, :, lo:hi])

    def drain(span):
        for i in range(tiles - 2, tiles):
            wait(dgu_copies(i, span, True))

    whole, da_s = (0, hidden), gu_s.at[0, :, :width]

    def back(i, last=False):
        rows = at_tile(i)
        if not last:
            @pl.when(i < tiles - 2)
            def _():
                start(dgu_copies(i + 2, whole, False))
            wait(dgu_copies(i + 1, whole, False))
            x = streamed(x_hbm, None, i)
        else:
            in_copy(x_hbm, i).wait()
            x = in_s[i % 2]
        wide, scale, _ = normed(x)
        h_s[rows, :] = outer(wide, scale, h_s[rows, :], da_s[...])
        if not last:
            da_s[...] = dot(dgu_s[lax.rem(i + 1, 2)], wgut[...])

    first, second = (0, half), (half, hidden)
    start(gu_in(0, first))
    loop({7: [(scatter_add, 1, 0, every)]}, lambda i: gate_up(i, first, a_hbm))
    start(gu_in(0, second))
    scatter_fill(0, D)
    drain(first)
    scatter_fill(0, FIRST)
    loop({4: [(scatter_add, 1, 1, every)], 6: [(scatter_add, 0, 0, D), (scatter_add, 0, 0, FIRST)]}, lambda i: gate_up(i, second, x_hbm))
    drain(second)
    for i in range(2):
        start(dgu_copies(i, whole, False))
    scatter_fill(0, SECOND)
    scatter_add(1, 2, every)
    wait(dgu_copies(0, whole, False))
    da_s[...] = dot(dgu_s[0], wgut[...])
    loop({0: [(scatter_add, 0, 1, D), (scatter_add, 0, 1, FIRST)],
          2: [(scatter_add, 1, 3, every), (scatter_add, 0, 0, SECOND)], 3: [(scatter_add, 0, 2, D), (scatter_add, 0, 2, FIRST)],
          4: [(scatter_add, 0, 1, SECOND)], 5: [(scatter_add, 0, 3, D), (scatter_add, 0, 3, FIRST)], 6: [(scatter_add, 0, 2, SECOND)]}, back, tiles - 1)
    back(tiles - 1, True)
    scatter_add(0, 3, SECOND)
    wait([result_copy(0, a) for a in every])


def pieces_of(hidden):
    lanes = hidden // 128
    cuts = [128 * -(-lanes * q // 4) for q in range(5)]
    return list(zip(cuts, cuts[1:]))


def solution(mesh):
    group = mesh.shape["dp"]
    side = math.isqrt(group)
    assert side * side == group == 2**STEPS

    def local(x, dy, w_gate, w_up, w_down):
        _, tokens, width = x.shape
        layers, share_gu, hidden = w_gate.shape
        share_d = w_down.shape[1]
        parts = [pltpu.VMEM((group, share_gu, hi - lo), bf16) for lo, hi in pieces_of(hidden) * 2]
        parts += [pltpu.VMEM((group, share_d, width // 4), bf16)] * 4
        any_, vmem = pl.BlockSpec(memory_space=pl.ANY), pl.BlockSpec(memory_space=pltpu.VMEM)
        shapes = ((tokens, width), w_gate.shape, w_up.shape, w_down.shape, (tokens, hidden), (tokens, 2 * hidden), (tokens, width))
        dma = pltpu.SemaphoreType.DMA
        out = pl.pallas_call(
            functools.partial(kernel, (tokens, width, hidden, share_gu, share_d)),
            out_shape=[jax.ShapeDtypeStruct(s, bf16) for s in shapes] + [jax.ShapeDtypeStruct((tokens, 2 * hidden), f32)],
            in_specs=[any_] * 5,
            out_specs=[vmem] + [any_] * 7,
            scratch_shapes=[
                pltpu.VMEM((2, TILE, width), bf16),
                pltpu.VMEM((2, TILE, 2 * pieces_of(hidden)[2][0]), f32),
                pltpu.VMEM((layers, width, 2 * hidden), bf16),
                pltpu.VMEM((2 * hidden, width), bf16),
                pltpu.VMEM((width, hidden), bf16),
                pltpu.VMEM((layers, width, 2 * hidden), f32),
                pltpu.VMEM((layers, hidden, width), f32),
                pltpu.VMEM((2, TILE, hidden), bf16),
                pltpu.VMEM((2, TILE, 2 * hidden), bf16),
            ] + parts * 2 + [
                dma((4, 12, STEPS)), dma((4, 12, STEPS)), dma((2, 12, STEPS)), dma((2, 12, STEPS)),
                pltpu.SemaphoreType.REGULAR((12, STEPS)), dma((2, 12)), dma((2,)), dma((2,)), dma((2,)), dma((2, 2)), dma((2, 2)),
            ],
            compiler_params=pltpu.CompilerParams(collective_id=0, has_side_effects=True, vmem_limit_bytes=VMEM_LIMIT),
            name="stack",
        )(x[0], dy[0], w_gate, w_up, w_down)
        return (out[0][None], *out[1:4])

    tokens_spec = P(("rep", "dp"), None, None)
    weight_spec, grad_spec = P(None, "dp", None), P("rep", "dp", None)
    return jax.shard_map(local, mesh=mesh, in_specs=(tokens_spec, tokens_spec) + (weight_spec,) * 3,
                         out_specs=(tokens_spec,) + (grad_spec,) * 3, check_vma=False)
```

time: 209 us -> 191 us (0.914)
  Pallas kernels: 202 us -> 184 us
    pallas_call x1, Pallas kernels: 202 us -> 184 us  [local(): pl.pallas_call(functools.partial(kernel, (tokens, width, hidden, share_gu...]
where the time goes in v3:
time: 191 us
  Pallas kernels  184 us (96%)
  local copies, waits for them, and re-layouts  6.55 us (3%)
    pallas_call x1, Pallas kernels, local(): pl.pallas_call(functools.partial(kernel, (tokens, width, hidden, share_gu...  184 us
    unnamed x10, local copies, waits for them, and re-layouts  6.55 us

profile of v3, /device:TPU:96, one launch (start us, length us, event | category | flops | bytes accessed | tf_op | source)
XLA Modules:
  0.0 191.0 jit_solution(12721026077590835490)
XLA Ops:
  0.6 183.7 %stack.1 = (bf16[4096,512]{1,0:T(8,128)(2,1)}, bf16[2,32,1408]{2,1,0:T(8,128)(2,1)}, bf16[2,32,1408]{2,1,0:T(8,128)(2,1)}, bf16[2,88,512]{2,1,0:T(8,128)(2,1)}, ...) custom-call(bf16[4096,512]{1,0:T(8,128)(2,1)} %bitcast.3, ...), custom_call_target="tpu_custom_call" | custom-call | tf_op jit(solution)/shard_map/stack/pallas_call | solution.py:446
  184.4 0.0 copy-start.2
  184.4 0.0 copy-start.1
  184.4 0.0 copy-start
  184.4 4.5 %copy.13 = bf16[1,4096,512]{2,1,0:T(8,128)(2,1)} copy(bf16[1,4096,512]{2,1,0:T(8,128)(2,1)} %bitcast.5) | data formatting | bytes 8388608
  188.9 0.0 copy-done.2
  188.9 0.7 copy.14
  189.6 0.0 copy-done.1
  189.6 0.7 copy.15
  190.3 0.0 copy-done
  190.3 0.7 copy.16
Async XLA Ops:
  184.4 4.6 %copy-start.2 = (bf16[2,32,1408]{2,1,0:T(8,128)(2,1)S(1)}, bf16[2,32,1408]{2,1,0:T(8,128)(2,1)}, u32[]{:S(2)}) copy-start(bf16[2,32,1408]{2,1,0:T(8,128)(2,1)} %get-tuple-element.17) | copy-start | bytes 540676
  184.4 5.2 %copy-start.1 = (bf16[2,32,1408]{2,1,0:T(8,128)(2,1)S(1)}, bf16[2,32,1408]{2,1,0:T(8,128)(2,1)}, u32[]{:S(2)}) copy-start(bf16[2,32,1408]{2,1,0:T(8,128)(2,1)} %get-tuple-element.18) | copy-start | bytes 540676
  184.4 5.9 %copy-start = (bf16[2,88,512]{2,1,0:T(8,128)(2,1)S(1)}, bf16[2,88,512]{2,1,0:T(8,128)(2,1)}, u32[]{:S(2)}) copy-start(bf16[2,88,512]{2,1,0:T(8,128)(2,1)} %get-tuple-element.19) | copy-start | bytes 540676

commit v4 on v3

v4 whole, which is shorter than its diff:
```python
import functools
import math

import jax
import jax.numpy as jnp
from jax import lax
from jax.experimental import pallas as pl
from jax.experimental.pallas import tpu as pltpu
from jax.sharding import PartitionSpec as P

bf16, f32 = jnp.bfloat16, jnp.float32
MESH = pl.DeviceIdType.MESH
TILE = 512
CHUNK = 256
STEPS = 4
GATHER = (((0, 1, 1, 1), (0, 2, 1, 2), (0, 3, 1, 3)), ((0, 4, 4, 4),), ((0, 8, 8, 8),))
SCATTER = (((8, 8, 8, 8),), ((4, 4, 4, 4),), ((1, 1, 1, 1), (2, 2, 1, 2), (3, 3, 1, 3)))
ROUNDS = 3
VMEM_LIMIT = 67043328
DIMS = ((1, 0), (0, 1), (3, 0), (0, 3))
PART = (0, 1, 0, 1, 2, 3, 2, 3, 0, 1, 2, 3)


def dot(a, b):
    return jnp.dot(a, b, preferred_element_type=f32)


def dot_t(a, b):
    return lax.dot_general(a, b, (((0,), (0,)), ((), ())), preferred_element_type=f32)


def flip(c, bits):
    return (c, c + 1 - 2 * lax.rem(c, 2), lax.rem(c + 2, 4), 3 - c)[bits]


def mask_of(part, slot):
    x = y = 0
    for bit in range(STEPS):
        if slot >> bit & 1:
            dx, dy = DIMS[(part + STEPS - 1 - bit) % 4]
            x, y = x ^ dx, y ^ dy
    return x, y


def kernel(sizes, x_hbm, dy_hbm, wg_hbm, wu_hbm, wd_hbm, dx_hbm, og_hbm, ou_hbm, od_hbm, p_hbm, dgu_hbm, a_hbm, gu_hbm, *scratch):
    (in_s, h_s, gu_s, wgu, wgut, wdt, acc_gu, acc_d, p_s, dgu_s, *rest) = scratch
    slots = (rest[:12], rest[12:24])
    send_sem, recv_sem, hand_send, hand_recv, credit, own_sem, in_sem, a_sem, p_sem, dgu_sem, gu_sem, dx_sem, ready = rest[24:]
    tokens, width, hidden, share_gu, share_d = sizes
    a_s = dgu_s.at[:, :, :width]
    wd0 = [(lo, min(lo + TILE, hidden), dgu_s.at[1, :min(TILE, hidden - lo), pl.ds((1 + lo // TILE) * width, width)]) for lo in range(0, hidden, TILE)]
    me, rep = lax.axis_index("dp"), lax.axis_index("rep")
    mx, my = lax.div(me, 4), lax.rem(me, 4)
    core = lax.rem(rep, 2)
    tiles = tokens // TILE

    def device(mask):
        return flip(mx, mask[0]) * 4 + flip(my, mask[1])

    def to(a, slot):
        return {"dp": device(mask_of(PART[a], slot))}

    partner = {"rep": rep + 1 - 2 * core}
    pieces = pieces_of(hidden)
    cols = pieces + [(hidden + lo, hidden + hi) for lo, hi in pieces] + [(width * q // 4, width * (q + 1) // 4) for q in range(4)]
    GU, D = range(8), range(8, 12)
    half = pieces[2][0]
    FIRST, SECOND = (0, 1, 4, 5), (2, 3, 6, 7)
    keeper = (0, 0, 0, 0, 1, 1, 1, 1, 0, 0, 1, 1)

    def in_copy(source, i):
        return pltpu.make_async_copy(source.at[at_tile(i)], in_s.at[lax.rem(i, 2)], in_sem.at[lax.rem(i, 2)])

    def streamed(source, following, i):
        @pl.when(i < tiles - 1)
        def _():
            in_copy(source, i + 1).start()
        if following is not None:
            @pl.when(i == tiles - 1)
            def _():
                in_copy(following, 0).start()
        in_copy(source, i).wait()
        return in_s[lax.rem(i, 2)]

    def at_tile(i):
        if isinstance(i, int):
            return pl.ds(i * TILE, TILE)
        return pl.ds(pl.multiple_of(i * TILE, TILE), TILE)

    def start(copies):
        for copy in copies:
            copy.start()

    def wait(copies):
        for copy in copies:
            copy.wait()

    def rows_of(a, slot):
        share = share_gu if a < 8 else share_d
        return pl.ds(pl.multiple_of(device(mask_of(PART[a], slot)) * share, 8), share)

    def own(layer, a, g, u, d):
        lo, hi = cols[a]
        return g.at[layer, :, lo:hi] if a < 4 else u.at[layer, :, lo - hidden:hi - hidden] if a < 8 else d.at[layer, :, lo:hi]

    def own_copy(layer, a):
        return pltpu.make_async_copy(own(layer, a, wg_hbm, wu_hbm, wd_hbm), slots[layer][a].at[0], own_sem.at[layer, a])

    def result_copy(layer, a):
        return pltpu.make_async_copy(slots[1][a].at[0], own(layer, a, og_hbm, ou_hbm, od_hbm), own_sem.at[layer, a])

    def exchange(kind, a, rounds, n, source, target):
        before = sum(len(r) for r in rounds[:n])
        return [pltpu.make_async_remote_copy(
            src_ref=source[a].at[pl.ds(here, count)], dst_ref=target[a].at[pl.ds(there, count)],
            send_sem=send_sem.at[kind, a, before + k], recv_sem=recv_sem.at[kind, a, before + k],
            device_id=to(a, slot), device_id_type=MESH) for k, (here, there, count, slot) in enumerate(rounds[n])]

    def gather_copies(layer, n, a):
        return exchange(layer, a, GATHER, n, slots[layer], slots[layer])

    def hand_copy(layer, n, a):
        there = slots[layer][a].at[pl.ds(*((1, 3), (4, 4), (8, 8))[n])]
        return pltpu.make_async_remote_copy(
            src_ref=there, dst_ref=there, send_sem=hand_send.at[layer, a, n], recv_sem=hand_recv.at[layer, a, n],
            device_id=partner, device_id_type=MESH)

    def by_core(arrays, act):
        for side in range(2):
            @pl.when(core == side)
            def _():
                act([a for a in arrays if keeper[a] == side], [a for a in arrays if keeper[a] != side])

    def gather_step(layer, n, arrays):
        def act(mine, _):
            for a in mine:
                if n > 0:
                    wait(gather_copies(layer, n - 1, a))
                if n < ROUNDS:
                    start(gather_copies(layer, n, a))
                if n > 0:
                    hand_copy(layer, n - 1, a).start()
        by_core(arrays, act)

    def gather_end(layer, arrays):
        def act(mine, others):
            for n in range(ROUNDS):
                for a in others:
                    hand_copy(layer, n, a).wait_recv()
                for a in mine:
                    hand_copy(layer, n, a).wait_send()
        by_core(arrays, act)

    def install(layer, arrays):
        for r in range(16):
            for a in arrays:
                lo, hi = cols[a]
                if a < 8:
                    wgu[layer, rows_of(a, r), lo:hi] = slots[layer][a][r]
                else:
                    acc_d[layer, rows_of(a, r), lo:hi] = slots[layer][a][r].astype(f32)

    def scatter_copies(layer, n, a):
        return exchange(2 + layer, a, SCATTER, n, slots[1], slots[0])

    def scatter_start(layer, n, arrays):
        for a in arrays:
            before = sum(len(r) for r in SCATTER[:n])
            for k, copy in enumerate(scatter_copies(layer, n, a)):
                if layer == 0:
                    pl.semaphore_wait(credit.at[a, before + k], 1)
                copy.start()

    def scatter_fill(layer, arrays):
        for a in arrays:
            lo, hi = cols[a]
            acc = acc_gu if a < 8 else acc_d
            for r in range(8, 16):
                slots[1][a][r] = acc[layer, rows_of(a, r), lo:hi].astype(bf16)
        scatter_start(layer, 0, arrays)

    def scatter_add(layer, n, arrays):
        keep, stay = ((8, 4), (4, 1), (1, 0))[n]
        for a in arrays:
            lo, hi = cols[a]
            acc = acc_gu if a < 8 else acc_d
            wait(scatter_copies(layer, n, a))
            for r in reversed(range(keep)):
                total = acc[layer, rows_of(a, r), lo:hi]
                for _, there, count, _ in SCATTER[n]:
                    if r < count:
                        total += slots[0][a][there + r].astype(f32)
                if n == ROUNDS - 1:
                    if layer == 0:
                        result_copy(1, a).wait()
                    slots[1][a][0] = total.astype(bf16)
                    result_copy(layer, a).start()
                elif r >= stay:
                    slots[1][a][r] = total.astype(bf16)
                else:
                    acc[layer, rows_of(a, r), lo:hi] = total
            if layer == 1:
                before = sum(len(r) for r in SCATTER[:n])
                for k, (_, _, _, slot) in enumerate(SCATTER[n]):
                    pl.semaphore_signal(credit.at[a, before + k], inc=1, device_id=to(a, slot), device_id_type=MESH)
        if n < ROUNDS - 1:
            scatter_start(layer, n + 1, arrays)

    def chunks_of(lo, hi):
        return [(at, min(at + CHUNK, hi)) for at in range(lo, hi, CHUNK)]

    def normed(h):
        wide = h.astype(f32)
        scale = lax.rsqrt(jnp.mean(wide * wide, -1, keepdims=True) + 1e-6)
        return wide, scale, (wide * scale).astype(bf16)

    def loop(events, body, n=tiles):
        def step(i, _):
            for when, actions in events.items():
                @pl.when(i == when)
                def _():
                    for act, *args in actions:
                        act(*args)
            body(i)
            return 0
        lax.fori_loop(0, n, step, 0)

    def transposes(layer, down):
        for lo in range(0, 2 * hidden, CHUNK):
            wgut[lo:lo + CHUNK, :] = wgu[layer, :, lo:lo + CHUNK].T
        for lo, hi, block in down:
            wdt[:, lo:hi] = block[...].T.astype(bf16)

    def inner(g, u, dq):
        dq = dq.astype(bf16).astype(f32)
        sig = 0.5 * jnp.tanh(0.5 * g) + 0.5
        s = g * sig
        return (s * u).astype(bf16), (dq * u * (sig + s * (1 - sig))).astype(bf16), (dq * s).astype(bf16)

    def outer(wide, scale, dy, da):
        da = da.astype(bf16).astype(f32)
        mean = jnp.mean(da * wide, -1, keepdims=True)
        return dy + (da * scale - wide * (mean * scale * scale * scale)).astype(bf16)

    every = range(12)
    for layer in range(2):
        start([own_copy(layer, a) for a in every])
    in_copy(x_hbm, 0).start()
    barrier = pltpu.get_barrier_semaphore()
    peers = [to(a, slot) for a in range(8, 12) for slot in (1, 3)]
    for peer in peers + [partner]:
        pl.semaphore_signal(barrier, inc=1, device_id=peer, device_id_type=MESH)
    wait([own_copy(0, a) for a in every])
    pl.semaphore_wait(barrier, 9)
    for n in range(ROUNDS):
        gather_step(0, n, GU)
        gather_step(0, n, D)
    wait([own_copy(1, a) for a in every])
    gather_step(1, 0, every)
    in_copy(x_hbm, 0).wait()
    a_s[0] = normed(in_s[0])[2]
    gather_step(0, ROUNDS, GU)
    gather_end(0, GU)
    install(0, GU)

    def p_out(i):
        return pltpu.make_async_copy(p_s.at[lax.rem(i, 2)], p_hbm.at[at_tile(i)], p_sem.at[lax.rem(i, 2)])

    def gu_out(i):
        return pltpu.make_async_copy(acc_gu.at[lax.rem(i, 2)], gu_hbm.at[at_tile(i)], gu_sem.at[lax.rem(i, 2), 0])

    def a_out(i):
        return pltpu.make_async_copy(a_s.at[lax.rem(i, 2)], a_hbm.at[at_tile(i)], a_sem.at[lax.rem(i, 2)])

    def next_x(i):
        slot = lax.rem(i + 1, 2)
        return pltpu.make_async_copy(x_hbm.at[at_tile(jnp.minimum(i + 1, tiles - 1))], in_s.at[slot], in_sem.at[slot])

    def down(slot):
        return sum(dot(p_s[slot, :, lo:hi], block[...]) for lo, hi, block in wd0).astype(bf16)

    def forward(i):
        slot = lax.rem(i, 2)
        next_x(i).start()
        a_out(i).start()

        @pl.when(i >= 1)
        def _():
            a_out(i - 1).wait()

        @pl.when(i >= 2)
        def _():
            p_out(i - 2).wait()
            gu_out(i - 2).wait()

        @pl.when(i == 1)
        def _():
            gather_step(0, ROUNDS, D)
            gather_end(0, D)
            install(0, D)
            for lo, hi, block in wd0:
                block[...] = acc_d[0, lo:hi].astype(bf16)
            for peer in peers:
                pl.semaphore_signal(ready, inc=1, device_id=peer, device_id_type=MESH)
        before = at_tile(jnp.maximum(i - 1, 0))
        h_s[before, :] += down(1 - slot)
        h_s[at_tile(i), :] = in_s[slot]
        a = a_s[slot]
        for lo, hi in chunks_of(0, hidden):
            g, u = dot(a, wgu[0, :, lo:hi]), dot(a, wgu[0, :, hidden + lo:hidden + hi])
            acc_gu[slot, :, lo:hi] = g
            acc_gu[slot, :, hidden + lo:hidden + hi] = u
            p_s[slot, :, lo:hi] = (g * (0.5 * jnp.tanh(0.5 * g) + 0.5) * u).astype(bf16)
        p_out(i).start()
        gu_out(i).start()
        next_x(i).wait()
        a_s[1 - slot] = normed(in_s[1 - slot])[2]

    loop({1: [(gather_step, 1, 1, every)], 3: [(gather_step, 1, 2, every)], 7: [(gather_step, 1, ROUNDS, every)]}, forward)
    h_s[at_tile(tiles - 1), :] += down((tiles - 1) % 2)
    a_out(tiles - 1).wait()
    in_copy(dy_hbm, 0).start()
    gather_end(1, every)
    install(1, every)
    transposes(1, [(lo, hi, acc_d.at[1, lo:hi]) for lo, hi in chunks_of(0, hidden)])
    acc_d[...] = jnp.zeros_like(acc_d)
    for i in (tiles - 2, tiles - 1):
        p_out(i).wait()
        gu_out(i).wait()
    acc_gu[...] = jnp.zeros_like(acc_gu)

    first, second = (0, half), (half, hidden)

    def gu_in(i, span):
        slot, n = lax.rem(i, 2), span[1] - span[0]
        return [pltpu.make_async_copy(gu_hbm.at[at_tile(i), pl.ds(side * hidden + span[0], n)], gu_s.at[slot, :, pl.ds(side * half, n)],
                                      gu_sem.at[slot, side]) for side in range(2)]

    def p_in(i):
        return pltpu.make_async_copy(p_hbm.at[at_tile(i)], p_s.at[lax.rem(i, 2)], p_sem.at[lax.rem(i, 2)])

    def last(i):
        rows = at_tile(i)
        wide, scale, a = normed(h_s[rows, :])
        dy = streamed(dy_hbm, a_hbm, i)
        for lo, hi in chunks_of(0, hidden):
            g, u = dot(a, wgu[1, :, lo:hi]), dot(a, wgu[1, :, hidden + lo:hidden + hi])
            p_s[0, :, lo:hi], dgu_s[0, :, lo:hi], dgu_s[0, :, hidden + lo:hidden + hi] = inner(g, u, dot(dy, wdt[:, lo:hi]))
        h_s[rows, :] = outer(wide, scale, dy, dot(dgu_s[0], wgut[...]))
        acc_d[1] += dot_t(p_s[0], dy)
        acc_gu[1] += dot_t(a, dgu_s[0])

    start(gu_in(0, first))
    loop({}, last)
    p_in(0).start()
    pl.semaphore_wait(ready, len(peers))
    for arrays in (FIRST, SECOND, D):
        scatter_fill(1, arrays)
    transposes(0, [(lo, min(lo + CHUNK, hi), block.at[lo - begin:min(lo + CHUNK, hi) - begin]) for begin, hi, block in wd0 for lo in range(begin, hi, CHUNK)])

    def dgu_copies(i, span, out):
        slot = lax.rem(i, 2)
        found = []
        for side in range(2):
            place = pl.ds(side * hidden + span[0], span[1] - span[0])
            there, here = dgu_hbm.at[at_tile(i), place], dgu_s.at[slot, :, place]
            found.append(pltpu.make_async_copy(*((here, there) if out else (there, here)), dgu_sem.at[slot, side, int(out)]))
        return found

    def gate_up(i, span, following, after, down=False):
        slot = lax.rem(i, 2)
        dy = h_s[at_tile(i), :]
        a = streamed(a_hbm, following, i)
        if down:
            @pl.when(i < tiles - 1)
            def _():
                p_in(i + 1).start()
            p_in(i).wait()

        @pl.when(i < tiles - 1)
        def _():
            start(gu_in(i + 1, span))

        @pl.when(i == tiles - 1)
        def _():
            after()

        @pl.when(i >= 2)
        def _():
            wait(dgu_copies(i - 2, span, True))
        wait(gu_in(i, span))
        if down:
            acc_d[0] += dot_t(p_s[slot], dy)
        for lo, hi in chunks_of(*span):
            here = [slice(at + lo - span[0], at + hi - span[0]) for at in (0, half)]
            _, dgu_s[slot, :, lo:hi], dgu_s[slot, :, hidden + lo:hidden + hi] = inner(gu_s[slot, :, here[0]], gu_s[slot, :, here[1]], dot(dy, wdt[:, lo:hi]))
        for side in range(2):
            lo, hi = (side * hidden + at for at in span)
            acc_gu[0, :, lo:hi] += dot_t(a, dgu_s[slot, :, lo:hi])
        start(dgu_copies(i, span, True))

    def drain(span):
        for i in range(tiles - 2, tiles):
            wait(dgu_copies(i, span, True))

    whole, da_s = (0, hidden), gu_s.at[0, :, :width]

    def x_in(i):
        tile = tiles - 1 - i
        return pltpu.make_async_copy(x_hbm.at[at_tile(tile)], in_s.at[lax.rem(i, 2)], in_sem.at[lax.rem(i, 2)])

    def dgu_in(i):
        return dgu_copies(tiles - 1 - i, whole, False)

    def dx_out(i):
        rows = at_tile(tiles - 1 - i)
        return pltpu.make_async_copy(h_s.at[rows], dx_hbm.at[rows], dx_sem.at[i])

    def back(i):
        rows = at_tile(tiles - 1 - i)
        if isinstance(i, int):
            x_in(i).wait()
            ahead = i < tiles - 1
        else:
            @pl.when(i < tiles - 2)
            def _():
                start(dgu_in(i + 2))

            @pl.when(i >= 1)
            def _():
                wait(dgu_in(i + 1))
            x_in(i + 1).start()
            x_in(i).wait()
            ahead = True
        wide, scale, _ = normed(in_s[i % 2 if isinstance(i, int) else lax.rem(i, 2)])
        h_s[rows, :] = outer(wide, scale, h_s[rows, :], da_s[...])
        dx_out(i).start()
        if ahead:
            da_s[...] = dot(dgu_s[lax.rem(tiles - 2 - i, 2)], wgut[...])

    loop({3: [(scatter_add, 1, 0, FIRST)], 4: [(scatter_add, 1, 0, SECOND)], 6: [(scatter_add, 1, 0, D), (scatter_add, 1, 1, FIRST)],
          7: [(scatter_add, 1, 1, SECOND)]}, lambda i: gate_up(i, first, a_hbm, lambda: start(gu_in(0, second)), True))
    scatter_add(1, 1, D)
    scatter_fill(0, D)
    drain(first)
    scatter_fill(0, FIRST)
    loop({1: [(scatter_add, 1, 2, FIRST)], 2: [(scatter_add, 1, 2, SECOND)], 3: [(scatter_add, 1, 2, D)], 5: [(scatter_add, 0, 0, D)],
          7: [(scatter_add, 0, 0, FIRST)]}, lambda i: gate_up(i, second, None, lambda: x_in(0).start()))
    drain(second)
    scatter_add(0, 1, D)
    scatter_fill(0, SECOND)
    da_s[...] = dot(dgu_s[(tiles - 1) % 2], wgut[...])
    loop({1: [(scatter_add, 0, 1, FIRST)], 2: [(scatter_add, 0, 2, D)], 3: [(scatter_add, 0, 0, SECOND)], 5: [(scatter_add, 0, 2, FIRST)],
          6: [(scatter_add, 0, 1, SECOND)]}, back, tiles - 1)
    back(tiles - 1)
    scatter_add(0, 2, SECOND)
    wait([dx_out(i) for i in range(tiles)])
    wait([result_copy(0, a) for a in every])


def pieces_of(hidden):
    lanes = hidden // 128
    cuts = [128 * -(-lanes * q // 4) for q in range(5)]
    return list(zip(cuts, cuts[1:]))


def solution(mesh):
    group = mesh.shape["dp"]
    side = math.isqrt(group)
    assert side * side == group == 2**STEPS

    def local(x, dy, w_gate, w_up, w_down):
        _, tokens, width = x.shape
        layers, share_gu, hidden = w_gate.shape
        share_d = w_down.shape[1]
        parts = [pltpu.VMEM((group, share_gu, hi - lo), bf16) for lo, hi in pieces_of(hidden) * 2]
        parts += [pltpu.VMEM((group, share_d, width // 4), bf16)] * 4
        any_, vmem = pl.BlockSpec(memory_space=pl.ANY), pl.BlockSpec(memory_space=pltpu.VMEM)
        shapes = ((tokens, width), w_gate.shape, w_up.shape, w_down.shape, (tokens, hidden), (tokens, 2 * hidden), (tokens, width))
        dma = pltpu.SemaphoreType.DMA
        out = pl.pallas_call(
            functools.partial(kernel, (tokens, width, hidden, share_gu, share_d)),
            out_shape=[jax.ShapeDtypeStruct(s, bf16) for s in shapes] + [jax.ShapeDtypeStruct((tokens, 2 * hidden), f32)],
            in_specs=[any_] * 5,
            out_specs=[any_] * 8,
            scratch_shapes=[
                pltpu.VMEM((2, TILE, width), bf16),
                pltpu.VMEM((tokens, width), bf16),
                pltpu.VMEM((2, TILE, 2 * pieces_of(hidden)[2][0]), f32),
                pltpu.VMEM((layers, width, 2 * hidden), bf16),
                pltpu.VMEM((2 * hidden, width), bf16),
                pltpu.VMEM((width, hidden), bf16),
                pltpu.VMEM((layers, width, 2 * hidden), f32),
                pltpu.VMEM((layers, hidden, width), f32),
                pltpu.VMEM((2, TILE, hidden), bf16),
                pltpu.VMEM((2, TILE, 2 * hidden), bf16),
            ] + parts * 2 + [
                dma((4, 12, 5)), dma((4, 12, 5)), dma((2, 12, ROUNDS)), dma((2, 12, ROUNDS)),
                pltpu.SemaphoreType.REGULAR((12, 5)), dma((2, 12)), dma((2,)), dma((2,)), dma((2,)), dma((2, 2, 2)), dma((2, 2)), dma((tokens // TILE,)),
                pltpu.SemaphoreType.REGULAR,
            ],
            compiler_params=pltpu.CompilerParams(collective_id=0, has_side_effects=True, vmem_limit_bytes=VMEM_LIMIT),
            name="stack",
        )(x[0], dy[0], w_gate, w_up, w_down)
        return (out[0][None], *out[1:4])

    tokens_spec = P(("rep", "dp"), None, None)
    weight_spec, grad_spec = P(None, "dp", None), P("rep", "dp", None)
    return jax.shard_map(local, mesh=mesh, in_specs=(tokens_spec, tokens_spec) + (weight_spec,) * 3,
                         out_specs=(tokens_spec,) + (grad_spec,) * 3, check_vma=False)
```

time: 191 us -> 185 us (0.969)
  Pallas kernels: 184 us -> 178 us
    pallas_call x1, Pallas kernels: 184 us -> 178 us  [local(): pl.pallas_call(functools.partial(kernel, (tokens, width, hidden, share_gu...]
where the time goes in v4:
time: 185 us
  Pallas kernels  178 us (96%)
  local copies, waits for them, and re-layouts  6.55 us (4%)
    pallas_call x1, Pallas kernels, local(): pl.pallas_call(functools.partial(kernel, (tokens, width, hidden, share_gu...  178 us
    unnamed x10, local copies, waits for them, and re-layouts  6.55 us

profile of v4, /device:TPU:96, one launch (start us, length us, event | category | flops | bytes accessed | tf_op | source)
XLA Modules:
  0.0 185.1 jit_solution(17515078186294015884)
XLA Ops:
  0.6 177.8 %stack.1 = (bf16[4096,512]{1,0:T(8,128)(2,1)}, bf16[2,32,1408]{2,1,0:T(8,128)(2,1)}, bf16[2,32,1408]{2,1,0:T(8,128)(2,1)}, bf16[2,88,512]{2,1,0:T(8,128)(2,1)}, ...) custom-call(bf16[4096,512]{1,0:T(8,128)(2,1)} %bitcast.3, ...), custom_call_target="tpu_custom_call" | custom-call | tf_op jit(solution)/shard_map/stack/pallas_call | solution.py:481
  178.5 0.0 copy-start.2
  178.5 0.0 copy-start.1
  178.5 0.0 copy-start
  178.5 4.5 %copy.13 = bf16[1,4096,512]{2,1,0:T(8,128)(2,1)} copy(bf16[1,4096,512]{2,1,0:T(8,128)(2,1)} %bitcast.5) | data formatting | bytes 8388608
  183.0 0.0 copy-done.2
  183.0 0.7 copy.14
  183.7 0.0 copy-done.1
  183.7 0.7 copy.15
  184.4 0.0 copy-done
  184.4 0.7 copy.16
Async XLA Ops:
  178.5 4.6 %copy-start.2 = (bf16[2,32,1408]{2,1,0:T(8,128)(2,1)S(1)}, bf16[2,32,1408]{2,1,0:T(8,128)(2,1)}, u32[]{:S(2)}) copy-start(bf16[2,32,1408]{2,1,0:T(8,128)(2,1)} %get-tuple-element.17) | copy-start | bytes 540676
  178.5 5.2 %copy-start.1 = (bf16[2,32,1408]{2,1,0:T(8,128)(2,1)S(1)}, bf16[2,32,1408]{2,1,0:T(8,128)(2,1)}, u32[]{:S(2)}) copy-start(bf16[2,32,1408]{2,1,0:T(8,128)(2,1)} %get-tuple-element.18) | copy-start | bytes 540676
  178.5 5.9 %copy-start = (bf16[2,88,512]{2,1,0:T(8,128)(2,1)S(1)}, bf16[2,88,512]{2,1,0:T(8,128)(2,1)}, u32[]{:S(2)}) copy-start(bf16[2,88,512]{2,1,0:T(8,128)(2,1)} %get-tuple-element.19) | copy-start | bytes 540676

commit v5 on v4

--- a/solution.py
+++ b/solution.py
@@ -308,9 +308,11 @@
         a = a_s[slot]
         for lo, hi in chunks_of(0, hidden):
             g, u = dot(a, wgu[0, :, lo:hi]), dot(a, wgu[0, :, hidden + lo:hidden + hi])
-            acc_gu[slot, :, lo:hi] = g
-            acc_gu[slot, :, hidden + lo:hidden + hi] = u
-            p_s[slot, :, lo:hi] = (g * (0.5 * jnp.tanh(0.5 * g) + 0.5) * u).astype(bf16)
+            sig = 0.5 * jnp.tanh(0.5 * g) + 0.5
+            s = g * sig
+            p_s[slot, :, lo:hi] = (s * u).astype(bf16)
+            acc_gu[slot, :, lo:hi] = u * (sig + s * (1 - sig))
+            acc_gu[slot, :, hidden + lo:hidden + hi] = s
         p_out(i).start()
         gu_out(i).start()
         next_x(i).wait()
@@ -393,7 +395,9 @@
             acc_d[0] += dot_t(p_s[slot], dy)
         for lo, hi in chunks_of(*span):
             here = [slice(at + lo - span[0], at + hi - span[0]) for at in (0, half)]
-            _, dgu_s[slot, :, lo:hi], dgu_s[slot, :, hidden + lo:hidden + hi] = inner(gu_s[slot, :, here[0]], gu_s[slot, :, here[1]], dot(dy, wdt[:, lo:hi]))
+            dq = dot(dy, wdt[:, lo:hi]).astype(bf16).astype(f32)
+            dgu_s[slot, :, lo:hi] = (dq * gu_s[slot, :, here[0]]).astype(bf16)
+            dgu_s[slot, :, hidden + lo:hidden + hi] = (dq * gu_s[slot, :, here[1]]).astype(bf16)
         for side in range(2):
             lo, hi = (side * hidden + at for at in span)
             acc_gu[0, :, lo:hi] += dot_t(a, dgu_s[slot, :, lo:hi])
@@ -438,24 +442,43 @@
         if ahead:
             da_s[...] = dot(dgu_s[lax.rem(tiles - 2 - i, 2)], wgut[...])
 
-    loop({3: [(scatter_add, 1, 0, FIRST)], 4: [(scatter_add, 1, 0, SECOND)], 6: [(scatter_add, 1, 0, D), (scatter_add, 1, 1, FIRST)],
-          7: [(scatter_add, 1, 1, SECOND)]}, lambda i: gate_up(i, first, a_hbm, lambda: start(gu_in(0, second)), True))
-    scatter_add(1, 1, D)
+    loop({3: [(scatter_add, 1, 0, FIRST)], 5: [(scatter_add, 1, 0, SECOND)], 6: [(scatter_add, 1, 0, D)], 7: [(scatter_add, 1, 1, FIRST)]},
+         lambda i: gate_up(i, first, a_hbm, lambda: start(gu_in(0, second)), True))
+    scatter_add(1, 1, SECOND)
     scatter_fill(0, D)
     drain(first)
     scatter_fill(0, FIRST)
-    loop({1: [(scatter_add, 1, 2, FIRST)], 2: [(scatter_add, 1, 2, SECOND)], 3: [(scatter_add, 1, 2, D)], 5: [(scatter_add, 0, 0, D)],
+    loop({1: [(scatter_add, 1, 1, D)], 3: [(scatter_add, 1, 2, FIRST)], 4: [(scatter_add, 1, 2, SECOND)], 5: [(scatter_add, 0, 0, D)],
           7: [(scatter_add, 0, 0, FIRST)]}, lambda i: gate_up(i, second, None, lambda: x_in(0).start()))
     drain(second)
-    scatter_add(0, 1, D)
     scatter_fill(0, SECOND)
+    scatter_add(1, 2, D)
     da_s[...] = dot(dgu_s[(tiles - 1) % 2], wgut[...])
-    loop({1: [(scatter_add, 0, 1, FIRST)], 2: [(scatter_add, 0, 2, D)], 3: [(scatter_add, 0, 0, SECOND)], 5: [(scatter_add, 0, 2, FIRST)],
-          6: [(scatter_add, 0, 1, SECOND)]}, back, tiles - 1)
+    loop({1: [(scatter_add, 0, 1, D)], 2: [(scatter_add, 0, 0, SECOND), (scatter_add, 0, 1, FIRST)], 4: [(scatter_add, 0, 2, D)],
+          5: [(scatter_add, 0, 1, SECOND), (scatter_add, 0, 2, FIRST)]}, back, tiles - 1)
     back(tiles - 1)
     scatter_add(0, 2, SECOND)
     wait([dx_out(i) for i in range(tiles)])
     wait([result_copy(0, a) for a in every])
+
+
+def hand_over(*refs):
+    n = len(refs) // 4
+    sources, targets, held, sems = refs[:n], refs[n:2 * n], refs[2 * n:3 * n], refs[3 * n:]
+    pairs = []
+    for k in range(n):
+        rows = sources[k].shape[0] // sems[k].shape[1]
+        for i in range(sems[k].shape[1]):
+            at = pl.ds(i * rows, rows)
+            pairs.append((pltpu.make_async_copy(sources[k].at[at], held[k].at[at], sems[k].at[0, i]),
+                          pltpu.make_async_copy(held[k].at[at], targets[k].at[at], sems[k].at[1, i])))
+    for into, _ in pairs:
+        into.start()
+    for into, out in pairs:
+        into.wait()
+        out.start()
+    for _, out in pairs:
+        out.wait()
 
 
 def pieces_of(hidden):
@@ -502,7 +525,16 @@
             compiler_params=pltpu.CompilerParams(collective_id=0, has_side_effects=True, vmem_limit_bytes=VMEM_LIMIT),
             name="stack",
         )(x[0], dy[0], w_gate, w_up, w_down)
-        return (out[0][None], *out[1:4])
+        shapes = [t.shape for t in out[:4]]
+        results = pl.pallas_call(
+            hand_over,
+            out_shape=[jax.ShapeDtypeStruct(s, bf16) for s in shapes],
+            in_specs=[any_] * 4,
+            out_specs=[any_] * 4,
+            scratch_shapes=[pltpu.VMEM(s, bf16) for s in shapes] + [dma((2, n)) for n in (8, 1, 1, 1)],
+            name="hand_over",
+        )(*out[:4])
+        return (results[0][None], *results[1:])
 
     tokens_spec = P(("rep", "dp"), None, None)
     weight_spec, grad_spec = P(None, "dp", None), P("rep", "dp", None)

time: 185 us -> 179 us (0.968)
  local copies, waits for them, and re-layouts: 6.55 us -> 0 us
    unnamed x10 -> x0, local copies, waits for them, and re-layouts: 6.55 us -> none
    pallas_call x1, Pallas kernels: 178 us -> 173 us  [local(): pl.pallas_call(functools.partial(kernel, (tokens, width, hidden, share_gu...]
    pallas_call x0 -> x1, Pallas kernels: none -> 4.06 us  [local(): pl.pallas_call(hand_over, out_shape=[jax.ShapeDtypeStruct(s, bf16) for s...]
where the time goes in v5:
time: 179 us; the launch traced here: 178 us
  Pallas kernels  177 us (99%)
    pallas_call x1, Pallas kernels, local(): pl.pallas_call(functools.partial(kernel, (tokens, width, hidden, share_gu...  173 us
    pallas_call x1, Pallas kernels, local(): pl.pallas_call(hand_over, out_shape=[jax.ShapeDtypeStruct(s, bf16) for s...  4.06 us

profile of v5, /device:TPU:96, one launch (start us, length us, event | category | flops | bytes accessed | tf_op | source)
XLA Modules:
  0.0 178.2 jit_solution(10191683774508241050)
XLA Ops:
  0.6 173.3 %stack.1 = (bf16[4096,512]{1,0:T(8,128)(2,1)}, bf16[2,32,1408]{2,1,0:T(8,128)(2,1)}, bf16[2,32,1408]{2,1,0:T(8,128)(2,1)}, bf16[2,88,512]{2,1,0:T(8,128)(2,1)}, ...) custom-call(bf16[4096,512]{1,0:T(8,128)(2,1)} %bitcast.3, ...), custom_call_target="tpu_custom_call" | custom-call | tf_op jit(solution)/shard_map/stack/pallas_call | solution.py:504
  173.9 4.1 %hand_over.1 = (bf16[4096,512]{1,0:T(8,128)(2,1)}, bf16[2,32,1408]{2,1,0:T(8,128)(2,1)}, bf16[2,32,1408]{2,1,0:T(8,128)(2,1)}, bf16[2,88,512]{2,1,0:T(8,128)(2,1)}) custom-call(bf16[4096,512]{1,0:T(8,128)(2,1)} %get-tuple-element.12.refs_0_, bf16[2,32,1408]{2,1,0:T(8,128)(2,1)} %get-tuple-element.13.refs_1_, bf16[2,32,1408]{2,1,0:T(8,128)(2,1)} %get-tuple-element.14.refs_2_, ...), custom_call_target="tpu_custom_call" | custom-call | tf_op jit(solution)/shard_map/hand_over/pallas_call | solution.py:529

commit v6 on v5

--- a/solution.py
+++ b/solution.py
@@ -43,7 +43,7 @@
 
 
 def kernel(sizes, x_hbm, dy_hbm, wg_hbm, wu_hbm, wd_hbm, dx_hbm, og_hbm, ou_hbm, od_hbm, p_hbm, dgu_hbm, a_hbm, gu_hbm, *scratch):
-    (in_s, h_s, gu_s, wgu, wgut, wdt, acc_gu, acc_d, p_s, dgu_s, *rest) = scratch
+    (in_s, h_s, gu_s, wgu, wgut, wdt, acc_gu, acc_d, p_s, dgu_s, tail, *rest) = scratch
     slots = (rest[:12], rest[12:24])
     send_sem, recv_sem, hand_send, hand_recv, credit, own_sem, in_sem, a_sem, p_sem, dgu_sem, gu_sem, dx_sem, ready = rest[24:]
     tokens, width, hidden, share_gu, share_d = sizes
@@ -214,6 +214,17 @@
         scale = lax.rsqrt(jnp.mean(wide * wide, -1, keepdims=True) + 1e-6)
         return wide, scale, (wide * scale).astype(bf16)
 
+    def tails(layer):
+        n = hidden % CHUNK
+        tail[layer, :, :n] = wgu[layer, :, hidden - n:hidden]
+        tail[layer, :, n:] = wgu[layer, :, 2 * hidden - n:]
+
+    def project(layer, a, lo, hi):
+        if hi - lo == CHUNK:
+            return dot(a, wgu[layer, :, lo:hi]), dot(a, wgu[layer, :, hidden + lo:hidden + hi])
+        both = dot(a, tail[layer])
+        return both[:, :hi - lo], both[:, hi - lo:]
+
     def loop(events, body, n=tiles):
         def step(i, _):
             for when, actions in events.items():
@@ -262,6 +273,7 @@
     gather_step(0, ROUNDS, GU)
     gather_end(0, GU)
     install(0, GU)
+    tails(0)
 
     def p_out(i):
         return pltpu.make_async_copy(p_s.at[lax.rem(i, 2)], p_hbm.at[at_tile(i)], p_sem.at[lax.rem(i, 2)])
@@ -307,7 +319,7 @@
         h_s[at_tile(i), :] = in_s[slot]
         a = a_s[slot]
         for lo, hi in chunks_of(0, hidden):
-            g, u = dot(a, wgu[0, :, lo:hi]), dot(a, wgu[0, :, hidden + lo:hidden + hi])
+            g, u = project(0, a, lo, hi)
             sig = 0.5 * jnp.tanh(0.5 * g) + 0.5
             s = g * sig
             p_s[slot, :, lo:hi] = (s * u).astype(bf16)
@@ -324,6 +336,7 @@
     in_copy(dy_hbm, 0).start()
     gather_end(1, every)
     install(1, every)
+    tails(1)
     transposes(1, [(lo, hi, acc_d.at[1, lo:hi]) for lo, hi in chunks_of(0, hidden)])
     acc_d[...] = jnp.zeros_like(acc_d)
     for i in (tiles - 2, tiles - 1):
@@ -346,13 +359,14 @@
         wide, scale, a = normed(h_s[rows, :])
         dy = streamed(dy_hbm, a_hbm, i)
         for lo, hi in chunks_of(0, hidden):
-            g, u = dot(a, wgu[1, :, lo:hi]), dot(a, wgu[1, :, hidden + lo:hidden + hi])
+            g, u = project(1, a, lo, hi)
             p_s[0, :, lo:hi], dgu_s[0, :, lo:hi], dgu_s[0, :, hidden + lo:hidden + hi] = inner(g, u, dot(dy, wdt[:, lo:hi]))
         h_s[rows, :] = outer(wide, scale, dy, dot(dgu_s[0], wgut[...]))
         acc_d[1] += dot_t(p_s[0], dy)
         acc_gu[1] += dot_t(a, dgu_s[0])
 
-    start(gu_in(0, first))
+    for i in range(2):
+        start(gu_in(i, first))
     loop({}, last)
     p_in(0).start()
     pl.semaphore_wait(ready, len(peers))
@@ -378,14 +392,6 @@
             def _():
                 p_in(i + 1).start()
             p_in(i).wait()
-
-        @pl.when(i < tiles - 1)
-        def _():
-            start(gu_in(i + 1, span))
-
-        @pl.when(i == tiles - 1)
-        def _():
-            after()
 
         @pl.when(i >= 2)
         def _():
@@ -403,6 +409,14 @@
             acc_gu[0, :, lo:hi] += dot_t(a, dgu_s[slot, :, lo:hi])
         start(dgu_copies(i, span, True))
 
+        @pl.when(i < tiles - 2)
+        def _():
+            start(gu_in(i + 2, span))
+
+        @pl.when(i >= tiles - 2)
+        def _():
+            after(i + 2 - tiles)
+
     def drain(span):
         for i in range(tiles - 2, tiles):
             wait(dgu_copies(i, span, True))
@@ -443,14 +457,15 @@
             da_s[...] = dot(dgu_s[lax.rem(tiles - 2 - i, 2)], wgut[...])
 
     loop({3: [(scatter_add, 1, 0, FIRST)], 5: [(scatter_add, 1, 0, SECOND)], 6: [(scatter_add, 1, 0, D)], 7: [(scatter_add, 1, 1, FIRST)]},
-         lambda i: gate_up(i, first, a_hbm, lambda: start(gu_in(0, second)), True))
+         lambda i: gate_up(i, first, a_hbm, lambda k: start(gu_in(k, second)), True))
     scatter_add(1, 1, SECOND)
     scatter_fill(0, D)
     drain(first)
     scatter_fill(0, FIRST)
     loop({1: [(scatter_add, 1, 1, D)], 3: [(scatter_add, 1, 2, FIRST)], 4: [(scatter_add, 1, 2, SECOND)], 5: [(scatter_add, 0, 0, D)],
-          7: [(scatter_add, 0, 0, FIRST)]}, lambda i: gate_up(i, second, None, lambda: x_in(0).start()))
+          7: [(scatter_add, 0, 0, FIRST)]}, lambda i: gate_up(i, second, None, lambda k: None))
     drain(second)
+    x_in(0).start()
     scatter_fill(0, SECOND)
     scatter_add(1, 2, D)
     da_s[...] = dot(dgu_s[(tiles - 1) % 2], wgut[...])
@@ -517,6 +532,7 @@
                 pltpu.VMEM((layers, hidden, width), f32),
                 pltpu.VMEM((2, TILE, hidden), bf16),
                 pltpu.VMEM((2, TILE, 2 * hidden), bf16),
+                pltpu.VMEM((layers, width, 2 * (hidden % CHUNK)), bf16),
             ] + parts * 2 + [
                 dma((4, 12, 5)), dma((4, 12, 5)), dma((2, 12, ROUNDS)), dma((2, 12, ROUNDS)),
                 pltpu.SemaphoreType.REGULAR((12, 5)), dma((2, 12)), dma((2,)), dma((2,)), dma((2,)), dma((2, 2, 2)), dma((2, 2)), dma((tokens // TILE,)),
@@ -531,7 +547,7 @@
             out_shape=[jax.ShapeDtypeStruct(s, bf16) for s in shapes],
             in_specs=[any_] * 4,
             out_specs=[any_] * 4,
-            scratch_shapes=[pltpu.VMEM(s, bf16) for s in shapes] + [dma((2, n)) for n in (8, 1, 1, 1)],
+            scratch_shapes=[pltpu.VMEM(s, bf16) for s in shapes] + [dma((2, n)) for n in (16, 1, 1, 1)],
             name="hand_over",
         )(*out[:4])
         return (results[0][None], *results[1:])

time: 179 us -> 177 us (0.989)
  Pallas kernels: 177 us -> 175 us
    pallas_call x1, Pallas kernels: 173 us -> 171 us  [local(): pl.pallas_call(functools.partial(kernel, (tokens, width, hidden, share_gu...]
where the time goes in v6:
time: 177 us; the launch traced here: 176 us
  Pallas kernels  175 us (99%)
    pallas_call x1, Pallas kernels, local(): pl.pallas_call(functools.partial(kernel, (tokens, width, hidden, share_gu...  171 us
    pallas_call x1, Pallas kernels, local(): pl.pallas_call(hand_over, out_shape=[jax.ShapeDtypeStruct(s, bf16) for s...  4.44 us

profile of v6, /device:TPU:96, one launch (start us, length us, event | category | flops | bytes accessed | tf_op | source)
XLA Modules:
  0.0 176.3 jit_solution(4229333447866101657)
XLA Ops:
  0.6 171.0 %stack.1 = (bf16[4096,512]{1,0:T(8,128)(2,1)}, bf16[2,32,1408]{2,1,0:T(8,128)(2,1)}, bf16[2,32,1408]{2,1,0:T(8,128)(2,1)}, bf16[2,88,512]{2,1,0:T(8,128)(2,1)}, ...) custom-call(bf16[4096,512]{1,0:T(8,128)(2,1)} %bitcast.3, ...), custom_call_target="tpu_custom_call" | custom-call | tf_op jit(solution)/shard_map/stack/pallas_call | solution.py:519
  171.6 4.4 %hand_over.1 = (bf16[4096,512]{1,0:T(8,128)(2,1)}, bf16[2,32,1408]{2,1,0:T(8,128)(2,1)}, bf16[2,32,1408]{2,1,0:T(8,128)(2,1)}, bf16[2,88,512]{2,1,0:T(8,128)(2,1)}) custom-call(bf16[4096,512]{1,0:T(8,128)(2,1)} %get-tuple-element.12.refs_0_, bf16[2,32,1408]{2,1,0:T(8,128)(2,1)} %get-tuple-element.13.refs_1_, bf16[2,32,1408]{2,1,0:T(8,128)(2,1)} %get-tuple-element.14.refs_2_, ...), custom_call_target="tpu_custom_call" | custom-call | tf_op jit(solution)/shard_map/hand_over/pallas_call | solution.py:545
